TPU v7x, 32 devices: a whole 2x2x4 slice. The times are simulated.
32 devices in a mesh: row: 4 (over x, core), col: 8 (over z, y).
Axes of the slice: x: 2, y: 2, z: 4, core: 2. Of those that a mesh axis runs over, the one named last changes fastest.
Arguments:
- tensor: float32 [1024, 32, 1024], P(None, 'row', 'col'), may hold values from -60 to 60, as said below
- factor_two: float32 [32, 32], P('row'), may hold values from -1 to 1
- factor_three: float32 [32, 32], P('col'), may hold values from -1 to 1
- factor_four: float32 [32, 16], replicated, may hold values from -1 to 1
- factor_init: float32 [1024, 64], replicated, may hold values from -6 to 6
Outputs:
- factor_new: float32 [1024, 64], replicated
- core: float32 [64, 32, 32, 16], P(None, 'row', 'col')
Inputs may be any that keep to these rules, and one draw needn't show every extreme that they name: `tensor`: scales vary from slab to slab.
All inputs are finite; a program needn't handle non-finite values.
Results may differ from a plain program's by a relative error of at most 0.00013.
Values sent between devices are 32-bit elements; how exact they have to be, the bound alone decides.
A program may use at most 128 MiB of HBM per device.

v0:
```python
import functools

import jax
import jax.numpy as jnp
from jax import lax
from jax.experimental import pallas as pl
from jax.experimental.pallas import tpu as pltpu
from jax.sharding import PartitionSpec as P

HIGHEST = lax.Precision.HIGHEST
LANES = 128


def dot(a, b, dims):
    return lax.dot_general(a, b, (dims, ((), ())), precision=HIGHEST, preferred_element_type=jnp.float32)


def inverse_factor(square):
    size = square.shape[0]
    rows = lax.broadcasted_iota(jnp.int32, (size, size), 0)
    cols = lax.broadcasted_iota(jnp.int32, (size, size), 1)
    index = lax.broadcasted_iota(jnp.int32, (size, 1), 0)
    left = square
    right = jnp.where(rows == cols, 1.0, 0.0).astype(jnp.float32)
    for k in range(size):
        scale = lax.rsqrt(left[k:k + 1, k:k + 1])
        column = left[:, k:k + 1] * scale
        pivot_left = left[k:k + 1, :] * scale
        pivot_right = right[k:k + 1, :] * scale
        factor = jnp.where(index > k, column, 0.0)
        left = left - factor * pivot_left
        right = jnp.where(index == k, pivot_right, right - factor * pivot_right)
    return right


def finish_kernel(image_ref, basis_ref, inverse_ref):
    image = image_ref[...]
    inverse = inverse_factor(dot(image, image, ((0,), (0,))))
    inverse_ref[...] = inverse
    basis_ref[...] = dot(image, inverse, ((1,), (1,)))


def finish(image):
    rank = image.shape[1]
    return pl.pallas_call(
        finish_kernel,
        out_shape=(
            jax.ShapeDtypeStruct(image.shape, jnp.float32),
            jax.ShapeDtypeStruct((rank, rank), jnp.float32),
        ),
    )(image)


def place():
    return lax.axis_index("row") * lax.axis_size("col") + lax.axis_index("col")


def greet(devices):
    cols = lax.axis_size("col")
    me = place()
    barrier = pltpu.get_barrier_semaphore()

    def hello(k, carry):
        peer = lax.rem(me + k, devices)
        pl.semaphore_signal(barrier, inc=1, device_id=(peer // cols, lax.rem(peer, cols)), device_id_type=pl.DeviceIdType.MESH)
        return carry

    lax.fori_loop(1, devices, hello, 0)
    pl.semaphore_wait(barrier, devices - 1)


def send_all(devices, source, target, send_sem, recv_sem):
    cols = lax.axis_size("col")
    me = place()

    def send(k, carry):
        peer = lax.rem(me + k, devices)
        pltpu.make_async_remote_copy(
            src_ref=source(peer),
            dst_ref=target.at[me],
            send_sem=send_sem,
            recv_sem=recv_sem,
            device_id=(peer // cols, lax.rem(peer, cols)),
            device_id_type=pl.DeviceIdType.MESH,
        ).start()
        return carry

    lax.fori_loop(1, devices, send, 0)
    whole = target.at[pl.ds(0, devices - 1)]
    pltpu.make_async_copy(whole, whole, send_sem).wait()
    pltpu.make_async_copy(whole, whole, recv_sem).wait()


def swap_kernel(devices, put_ref, out_ref, held, send_sem, recv_sem):
    me = place()
    greet(devices)
    send_all(devices, lambda peer: put_ref.at[peer], held, send_sem, recv_sem)
    held[me] = put_ref[me]
    out_ref[...] = held[...]


def total_kernel(devices, put_ref, out_ref, held, mine, spread, sems):
    me = place()
    greet(devices)
    send_all(devices, lambda peer: put_ref.at[peer], held, sems.at[0], sems.at[1])
    held[me] = put_ref[me]
    mine[...] = jnp.sum(held[...], axis=0)
    send_all(devices, lambda peer: mine, spread, sems.at[2], sems.at[3])
    spread[me] = mine[...]
    out_ref[...] = spread[...]


def swap(values, ident):
    devices = values.shape[0]
    return pl.pallas_call(
        functools.partial(swap_kernel, devices),
        out_shape=jax.ShapeDtypeStruct(values.shape, jnp.float32),
        in_specs=[pl.BlockSpec(memory_space=pltpu.VMEM)],
        out_specs=pl.BlockSpec(memory_space=pltpu.VMEM),
        scratch_shapes=[pltpu.VMEM(values.shape, jnp.float32), pltpu.SemaphoreType.DMA, pltpu.SemaphoreType.DMA],
        compiler_params=pltpu.CompilerParams(collective_id=ident, has_side_effects=True),
    )(values)


def total(values, ident):
    devices = values.shape[0]
    return pl.pallas_call(
        functools.partial(total_kernel, devices),
        out_shape=jax.ShapeDtypeStruct(values.shape, jnp.float32),
        in_specs=[pl.BlockSpec(memory_space=pltpu.VMEM)],
        out_specs=pl.BlockSpec(memory_space=pltpu.VMEM),
        scratch_shapes=[
            pltpu.VMEM(values.shape, jnp.float32),
            pltpu.VMEM(values.shape[1:], jnp.float32),
            pltpu.VMEM(values.shape, jnp.float32),
            pltpu.SemaphoreType.DMA((4,)),
        ],
        compiler_params=pltpu.CompilerParams(collective_id=ident, has_side_effects=True),
    )(values)


def shards(tensor, factor_two, factor_three, factor_four, factor_init):
    axes = ("row", "col")
    first_len, local_two, width = tensor.shape
    fourth_len, rank_four = factor_four.shape
    local_three = width // fourth_len
    rank_one = factor_init.shape[1]
    rows, cols = lax.axis_size("row"), lax.axis_size("col")
    devices = rows * cols
    local_pairs = local_two * local_three
    features = rank_four * rank_one
    part = features // devices
    data = tensor.reshape(first_len, local_pairs, fourth_len)
    rank_two, rank_three = factor_two.shape[1], factor_three.shape[1]

    def pull(vectors):
        mixed = jnp.einsum("apd,ar->prd", data, vectors, precision=lax.Precision.HIGH)
        return jnp.einsum("prd,de->per", mixed, factor_four, precision=HIGHEST).reshape(local_pairs, features)

    def share(values, ident):
        length = values.shape[1]
        padded = -(-length // LANES) * LANES
        values = jnp.pad(values, ((0, 0), (0, padded - length))).reshape(devices, padded // LANES, LANES)
        return swap(values, ident).reshape(devices, padded)[:, :length]

    def spread(block, ident, extra=None):
        put = block.reshape(local_pairs, devices, part).transpose(1, 0, 2).reshape(devices, local_pairs * part)
        if extra is not None:
            put = jnp.concatenate([put, jnp.broadcast_to(extra[None], (devices, extra.shape[0]))], axis=1)
        got = share(put, ident)
        rest = got[:, local_pairs * part:]
        got = got[:, :local_pairs * part]
        got = got.reshape(rows, cols, local_two, local_three, part)
        return got.transpose(0, 2, 1, 3, 4).reshape(rows * local_two, cols * local_three, part), rest

    def gather(block, ident):
        two, three, _ = block.shape
        put = block.reshape(rows, two // rows, cols, three // cols, part).transpose(0, 2, 1, 3, 4)
        got = share(put.reshape(devices, -1), ident).reshape(devices, (two // rows) * (three // cols), part)
        return got.transpose(1, 0, 2).reshape(got.shape[1], features)

    extra = jnp.concatenate([factor_two.reshape(-1), factor_three.reshape(-1)])
    block, rest = spread(pull(factor_init), 1, extra)
    rest = rest.reshape(rows, cols, -1)
    whole_two = rest[:, 0, :factor_two.size].reshape(-1, rank_two)
    whole_three = rest[0, :, factor_two.size:].reshape(-1, rank_three)
    block = jnp.einsum("bcq,bg->gcq", block, whole_two, precision=HIGHEST)
    block = jnp.einsum("gcq,cf->gfq", block, whole_three, precision=HIGHEST)
    block = jnp.einsum("gfq,cf->gcq", block, whole_three, precision=HIGHEST)
    block = jnp.einsum("gcq,bg->bcq", block, whole_two, precision=HIGHEST)
    block = gather(block, 2).reshape(local_pairs, rank_four, rank_one)
    block = jnp.einsum("per,de->pdr", block, factor_four, precision=HIGHEST)
    image = jnp.dot(tensor.reshape(first_len, -1), block.reshape(-1, rank_one), precision=lax.Precision.HIGH)
    half = first_len // 2
    image = jnp.concatenate([image[:half], image[half:]], axis=1).reshape(devices, half // devices, 2 * rank_one)
    image = total(image, 0).reshape(half, 2 * rank_one)
    image = jnp.concatenate([image[:, :rank_one], image[:, rank_one:]], axis=0)
    basis, inverse = finish(image)
    block, _ = spread(pull(image), 3)
    block = jnp.einsum("bcq,bg->gcq", block, whole_two, precision=HIGHEST)
    block = jnp.einsum("gcq,cf->gfq", block, whole_three, precision=HIGHEST)
    block = gather(block, 4).reshape(-1, rank_four, rank_one)
    core = jnp.einsum("per,sr->spe", block, inverse, precision=HIGHEST)
    return (basis, core.reshape(rank_one, rank_two // rows, rank_three // cols, rank_four))


def solution(mesh):
    in_specs = (P(None, "row", "col"), P("row", None), P("col", None), P(), P())
    out_specs = (P(), P(None, "row", "col", None))
    return jax.shard_map(shards, mesh=mesh, in_specs=in_specs, out_specs=out_specs, check_vma=False)
```

profile of v0, /device:TPU:0, one launch (start us, length us, event | category | flops | bytes accessed | tf_op | source)
XLA Modules:
  0.0 118.0 jit_solution(10538729618314387405)
XLA Ops:
  0.6 0.0 copy-start
  0.6 0.8 reshape.75
  1.5 0.8 reshape.74
  2.2 5.4 %copy.17 = f32[1024,8,128]{0,2,1:T(8,128)} copy(f32[1024,8,128]{2,1,0:T(8,128)} %param.5) | data formatting | bytes 8388608 | tf_op args[0]
  7.7 0.0 copy-start.1
  7.7 0.0 copy-done
  7.7 4.0 %fusion.21 = f32[64,1024]{0,1:S(1)} fusion(f32[1024,64]{0,1:T(8,128)S(1)} %copy-done, f32[1024,1024]{0,1:T(8,128)} %bitcast.94), kind=kOutput, calls=%fused_computation.32 | convolution fusion | flops 402653184 | bytes 4718592
  11.6 0.0 copy-done.1
  11.7 0.4 convolution_bitcast_fusion.3
  12.1 0.1 reshape_reshape.19
  12.2 0.3 copy.18
  12.5 0.2 reshape.73
  12.8 0.7 reshape.76.put_ref
  13.5 13.9 %shard_map.68 = f32[32,11,128]{2,1,0:T(8,128)} custom-call(f32[32,11,128]{2,1,0:T(8,128)} %reshape.76.put_ref), custom_call_target="tpu_custom_call" | custom-call | tf_op jit(solution)/shard_map/pallas_call | solution.py:115
  27.5 1.0 copy.53
  28.5 0.1 reshape.93
  28.6 0.1 reshape.95
  28.7 0.1 reshape.94
  28.8 0.1 reshape_squeeze.6
  28.8 0.3 reshape.79
  29.1 0.1 copy.19
  29.2 0.6 fusion.22
  29.8 0.9 convolution_bitcast_fusion.1
  30.7 0.6 fusion.23
  31.3 0.4 copy.20
  31.7 2.5 %convolution_bitcast_fusion = f32[4,8,8,4,32]{4,2,3,1,0:T(8,128)S(1)} fusion(f32[8,4,32,32]{3,2,1,0:T(8,128)S(1)} %copy.20, f32[4,8,32,1,1]{2,1,0,3,4:T(8,128)S(1)} %reshape.95), kind=kOutput, calls=%fused_computation.3 | convolution fusion | flops 12582912 | bytes 266240 | tf_op jit(solution)/shard_map/gcq,bg->bcq/dot_general | solution.py:190
  34.2 0.1 copy.21
  34.3 0.9 reshape.81.put_ref
  35.2 9.7 %shard_map.69 = f32[32,8,128]{2,1,0:T(8,128)} custom-call(f32[32,8,128]{2,1,0:T(8,128)} %reshape.81.put_ref), custom_call_target="tpu_custom_call" | custom-call | tf_op jit(solution)/shard_map/pallas_call | solution.py:115
  45.0 1.1 reshape_reshape.20
  46.0 0.3 copy.22
  46.4 0.1 reshape_reshape.21
  46.5 0.6 fusion.15
  47.1 4.7 %fusion.3 = f32[1024,64]{0,1:T(8,128)S(1)} fusion(f32[1024,64]{1,0:T(8,128)S(1)} %bitcast.99, f32[128,8,8,128]{3,2,1,0:T(8,128)} %bitcast.96), kind=kOutput, calls=%fused_computation.5 | convolution fusion | flops 402653184 | bytes 4718592 | tf_op jit(solution)/shard_map/dot_general | solution.py:193
  51.9 0.8 copy.23
  52.7 21.2 %shard_map.70 = f32[32,16,128]{2,1,0:T(8,128)} custom-call(f32[32,16,128]{2,1,0:T(8,128)} %bitcast.111), custom_call_target="tpu_custom_call" | custom-call | tf_op jit(solution)/shard_map/pallas_call | solution.py:127
  74.0 1.2 fusion.19
  75.1 4.0 %fusion.18 = f32[64,1024]{0,1:S(1)} fusion(f32[1024,1024]{0,1:T(8,128)} %bitcast.95, f32[512,64]{1,0:T(8,128)S(1)} %get-tuple-element.11, f32[512,64]{1,0:T(8,128)S(1)} %get-tuple-element.10), kind=kOutput, calls=%fused_computation.29 | convolution fusion | flops 402718720 | bytes 4718592
  79.2 0.8 pad_maximum_fusion.image_ref
  80.0 0.4 convolution_bitcast_fusion.2
  80.4 8.2 %shard_map.71 = (f32[1024,64]{1,0:T(8,128)}, f32[64,64]{1,0:T(8,128)}) custom-call(f32[1024,64]{1,0:T(8,128)} %pad_maximum_fusion.image_ref), custom_call_target="tpu_custom_call" | custom-call | tf_op jit(solution)/shard_map/pallas_call | solution.py:45
  88.6 1.9 %copy.29 = f32[1024,64]{0,1:T(8,128)} copy(f32[1024,64]{1,0:T(8,128)} %get-tuple-element.8) | data formatting | bytes 524288
  90.5 0.1 reshape_reshape.22
  90.7 0.3 copy.52
  91.0 0.8 reshape.86.put_ref
  91.8 10.3 %shard_map.72 = f32[32,8,128]{2,1,0:T(8,128)} custom-call(f32[32,8,128]{2,1,0:T(8,128)} %reshape.86.put_ref), custom_call_target="tpu_custom_call" | custom-call | tf_op jit(solution)/shard_map/pallas_call | solution.py:115
  102.1 0.0 copy-start.2
  102.1 1.2 reshape_reshape.23
  103.3 0.1 copy.25
  103.4 0.6 fusion.24
  104.0 0.9 fusion.7
  104.9 0.1 copy.51
  105.0 0.9 reshape.89.put_ref
  105.9 9.5 %shard_map.73 = f32[32,8,128]{2,1,0:T(8,128)} custom-call(f32[32,8,128]{2,1,0:T(8,128)} %reshape.89.put_ref), custom_call_target="tpu_custom_call" | custom-call | tf_op jit(solution)/shard_map/pallas_call | solution.py:115
  115.4 1.1 reshape_reshape.24
  116.5 0.3 copy.28
  116.8 0.1 dot_general.65
  117.0 0.0 copy-done.2
  117.0 1.1 fusion.10
  (8 shorter events, 0.1 us)
Async XLA Ops:
  0.6 7.0 %copy-start = (f32[1024,64]{0,1:T(8,128)S(1)}, f32[1024,64]{0,1:T(8,128)}, u32[]{:S(2)}) copy-start(f32[1024,64]{0,1:T(8,128)} %param.9) | copy-start | bytes 786436
  7.7 4.0 %copy-start.1 = (f32[32,16]{0,1:T(8,128)S(1)}, f32[32,16]{0,1:T(8,128)}, u32[]{:S(2)}) copy-start(f32[32,16]{0,1:T(8,128)} %param.8) | copy-start | bytes 6148
  102.1 14.9 %copy-start.2 = (f32[64,64]{1,0:T(8,128)S(1)}, f32[64,64]{1,0:T(8,128)}, u32[]{:S(2)}) copy-start(f32[64,64]{1,0:T(8,128)} %get-tuple-element.5) | copy-start | bytes 49156
where the time goes:
time: 119 us; the launch traced here: 118 us
  Pallas kernels  72.9 us (61%)
  local copies, waits for them, and re-layouts  22.1 us (19%)
  matrix products  21.3 us (18%)
    pallas_call x4, Pallas kernels, swap(): pl.pallas_call(functools.partial(swap_kernel, devices), out_shape=jax.Sha...  43.5 us
    pallas_call x1, Pallas kernels, total(): pl.pallas_call(functools.partial(total_kernel, devices), out_shape=jax.Sh...  21.2 us
    unnamed x9, local copies, waits for them, and re-layouts  8.38 us
    pallas_call x1, Pallas kernels, finish(): pl.pallas_call(finish_kernel, out_shape=(jax.ShapeDtypeStruct(image.shape...  8.18 us
    unnamed x2, matrix products  8 us
    dot_general x1, matrix products, shards(): jnp.dot(tensor.reshape(first_len, -1), block.reshape(-1, rank_one), preci...  4.73 us
    reshape x4, local copies, waits for them, and re-layouts, share(): jnp.pad(values, ((0, 0), (0, padded - length)))  3.39 us
    dot_general x1, matrix products, shards(): block = jnp.einsum('gcq,bg->bcq', block, whole_two, precision=HIGHEST)  2.48 us

commit v1 on v0

--- a/solution.py
+++ b/solution.py
@@ -139,7 +139,335 @@
     )(values)
 
 
+def split(x):
+    high = x.astype(jnp.bfloat16)
+    return high, (x - high.astype(jnp.float32)).astype(jnp.bfloat16)
+
+
+def narrow(a, b, dims=((1,), (0,))):
+    return lax.dot_general(a, b, (dims, ((), ())), preferred_element_type=jnp.float32)
+
+
+def left_split(x, high, low):
+    rows = x.shape[0]
+    top, rest = split(x)
+    both = narrow(jnp.concatenate([top, rest], axis=0), high)
+    return both[:rows] + both[rows:] + narrow(top, low)
+
+
+def iota(shape, dim):
+    return lax.broadcasted_iota(jnp.int32, shape, dim)
+
+
+def ones_where(mask):
+    return jnp.where(mask, 1.0, 0.0).astype(jnp.float32)
+
+
+def expand_rows(square, copies):
+    size = square.shape[0] * copies
+    pick = ones_where(iota((size, square.shape[0]), 0) // copies == iota((size, square.shape[0]), 1))
+    pick_right = ones_where(iota((square.shape[1], square.shape[1] * copies), 1) // copies == iota((square.shape[1], square.shape[1] * copies), 0))
+    wide = dot(dot(pick, square, ((1,), (0,))), pick_right, ((1,), (0,)))
+    return jnp.where(iota(wide.shape, 0) % copies == iota(wide.shape, 1) % copies, wide, 0.0)
+
+
+def store_lanes(matrix, copies, high_ref, low_ref):
+    width = matrix.shape[1] * copies
+    pick = ones_where(iota((matrix.shape[1], width), 1) // copies == iota((matrix.shape[1], width), 0))
+    wide = dot(matrix, pick, ((1,), (0,)))
+    keep = iota((copies, width), 1) % copies == iota((copies, width), 0)
+    for k in range(matrix.shape[0]):
+        rows = jnp.where(keep, jnp.broadcast_to(wide[k:k + 1, :], (copies, width)), 0.0)
+        high, low = split(rows)
+        high_ref[k * copies:(k + 1) * copies, :] = high
+        low_ref[k * copies:(k + 1) * copies, :] = low
+
+
+def send_to(source, target, peer, send_sem, recv_sem):
+    cols = lax.axis_size("col")
+    pltpu.make_async_remote_copy(
+        src_ref=source,
+        dst_ref=target,
+        send_sem=send_sem,
+        recv_sem=recv_sem,
+        device_id=(peer // cols, lax.rem(peer, cols)),
+        device_id_type=pl.DeviceIdType.MESH,
+    ).start()
+
+
+def wait_all(ref, count, sem):
+    whole = ref.at[pl.ds(0, count)]
+    pltpu.make_async_copy(whole, whole, sem).wait()
+
+
+def hooi_kernel(devices, tensor_ref, two_ref, three_ref, four_ref, init_ref, core_ref, basis_ref,
+                slabs, high_ref, low_ref, mix_high, mix_low, hat_high, hat_low, turn_high, turn_low,
+                lane_high, lane_low, twos, threes, puts, gots, put_image, got_image, mine, spread,
+                load_sem, send_sem, recv_sem, axis_sem):
+    rows, cols = lax.axis_size("row"), lax.axis_size("col")
+    row, col = lax.axis_index("row"), lax.axis_index("col")
+    me = place()
+    rank_one, first_len = init_ref.shape
+    local_two, local_three = two_ref.shape[0], three_ref.shape[0]
+    rank_four, fourth_len = four_ref.shape
+    width = local_three * fourth_len
+    lanes = local_two * rank_four
+    pairs = local_two * local_three
+    copies = rank_one // devices
+    features = pairs * rank_four
+    tile = local_three * copies
+
+    loads = [pltpu.make_async_copy(tensor_ref.at[:, b, :], slabs.at[b], load_sem.at[b]) for b in range(local_two)]
+    for load in loads:
+        load.start()
+
+    barrier = pltpu.get_barrier_semaphore()
+
+    def hello(k, carry):
+        peer = lax.rem(me + k, devices)
+        pl.semaphore_signal(barrier, inc=1, device_id=(peer // cols, lax.rem(peer, cols)), device_id_type=pl.DeviceIdType.MESH)
+        return carry
+
+    lax.fori_loop(1, devices, hello, 0)
+
+    lane = iota((fourth_len, features), 1)
+    pick = ones_where(iota((rank_four, features), 1) % rank_four == iota((rank_four, features), 0))
+    four = dot(four_ref[...], pick, ((0,), (0,)))
+    four_high = four.astype(jnp.bfloat16).astype(jnp.float32)
+    four_low = four - four_high
+    for b in range(local_two):
+        for c in range(local_three):
+            keep = lane // rank_four == c * local_two + b
+            part = slice((b * local_three + c) * fourth_len, (b * local_three + c + 1) * fourth_len)
+            mix_high[part, :] = jnp.where(keep, four_high, 0.0).astype(jnp.bfloat16)
+            mix_low[part, :] = jnp.where(keep, four_low, 0.0).astype(jnp.bfloat16)
+
+    init_high, init_low = split(init_ref[...])
+    init_both = jnp.concatenate([init_high, init_low], axis=0)
+    pulled = []
+    step = 2 if local_two % 2 == 0 else 1
+    for b in range(0, local_two, step):
+        for k in range(b, b + step):
+            loads[k].wait()
+            high, low = split(slabs[k])
+            high_ref[:, k * width:(k + 1) * width] = high
+            low_ref[:, k * width:(k + 1) * width] = low
+        part = slice(b * width, (b + step) * width)
+        both = narrow(init_both, high_ref[:, part])
+        pulled.append(both[:rank_one] + both[rank_one:] + narrow(init_high, low_ref[:, part]))
+    vectors = left_split(jnp.concatenate(pulled, axis=1), mix_high[...], mix_low[...])
+
+    def deal(vectors, put):
+        for c in range(local_three):
+            for k in range(copies):
+                put[pl.ds(c * copies + k, devices, stride=tile), :] = vectors[k * devices:(k + 1) * devices, c * lanes:(c + 1) * lanes]
+
+    def collect(got):
+        return jnp.concatenate([
+            jnp.concatenate([got[pl.ds(c * copies + k, devices, stride=tile), :] for k in range(copies)], axis=0)
+            for c in range(local_three)], axis=1)
+
+    def exchange(stage):
+        put, got = puts.at[stage], gots.at[stage]
+
+        def send(k, carry):
+            peer = lax.rem(me + k, devices)
+            send_to(put.at[pl.ds(pl.multiple_of(peer * tile, tile), tile)], got.at[pl.ds(pl.multiple_of(me * tile, tile), tile)], peer, send_sem.at[stage], recv_sem.at[stage])
+            return carry
+
+        lax.fori_loop(1, devices, send, 0)
+        here = pl.ds(pl.multiple_of(me * tile, tile), tile)
+        got[here, :] = put[here, :]
+
+    def arrive(stage):
+        wait_all(gots.at[stage], (devices - 1) * tile, recv_sem.at[stage])
+
+    def block(stage):
+        got = gots.at[stage]
+        return jnp.concatenate([got[k * cols * tile:(k + 1) * cols * tile, :] for k in range(rows)], axis=1)
+
+    def contract(stage, matrix):
+        high, low = split(matrix)
+        both = jnp.concatenate([high, low], axis=0)
+        size = matrix.shape[0]
+        top, rest = split(block(stage))
+        mixed = narrow(both, top)
+        mixed = mixed[:size] + mixed[size:] + narrow(high, rest)
+        return left_split(mixed, lane_high[...], lane_low[...])
+
+    def lay(result, stage):
+        for k in range(rows):
+            puts[stage, k * cols * tile:(k + 1) * cols * tile, :] = result[:, k * lanes:(k + 1) * lanes]
+
+    deal(vectors, puts.at[0])
+    pl.semaphore_wait(barrier, devices - 1)
+
+    def send_two(k, carry):
+        other = lax.rem(row + k, rows)
+        send_to(two_ref, twos.at[row], other * cols + col, axis_sem.at[0], axis_sem.at[1])
+        return carry
+
+    def send_three(k, carry):
+        other = lax.rem(col + k, cols)
+        send_to(three_ref, threes.at[col], row * cols + other, axis_sem.at[2], axis_sem.at[3])
+        return carry
+
+    lax.fori_loop(1, rows, send_two, 0)
+    lax.fori_loop(1, cols, send_three, 0)
+    exchange(0)
+    twos[row] = two_ref[...]
+    threes[col] = three_ref[...]
+
+    count = 4
+    piece = first_len // count
+    for k in range(count):
+        part = slice(k * piece, (k + 1) * piece)
+        hat = narrow(high_ref[part, :], mix_high[...]) + narrow(high_ref[part, :], mix_low[...]) + narrow(low_ref[part, :], mix_high[...])
+        high, low = split(hat)
+        hat_high[part, :] = high
+        hat_low[part, :] = low
+        turned = hat.T
+        high, low = split(turned)
+        turn_high[:, part] = high
+        turn_low[:, part] = low
+
+    wait_all(twos, rows - 1, axis_sem.at[1])
+    wait_all(threes, cols - 1, axis_sem.at[3])
+    whole_two = jnp.concatenate([twos[k] for k in range(rows)], axis=0)
+    whole_three = jnp.concatenate([threes[k] for k in range(cols)], axis=0)
+    store_lanes(dot(whole_two, whole_two, ((1,), (1,))), rank_four, lane_high, lane_low)
+    left = expand_rows(dot(whole_three, whole_three, ((1,), (1,))), copies)
+
+    arrive(0)
+    lay(contract(0, left), 1)
+    exchange(1)
+    store_lanes(whole_two, rank_four, lane_high, lane_low)
+    left = expand_rows(whole_three.T, copies)
+    arrive(1)
+
+    image = left_split(collect(gots.at[1]), turn_high[...], turn_low[...])
+    high_tiles = rank_one // 8
+    wide_tiles = first_len // LANES
+    each = high_tiles * wide_tiles // devices
+    spans = wide_tiles // each
+    for i in range(devices):
+        for j in range(each):
+            r, w = i // spans, (i % spans) * each + j
+            put_image[i, j] = image[r * 8:(r + 1) * 8, w * LANES:(w + 1) * LANES]
+
+    def scatter(k, carry):
+        peer = lax.rem(me + k, devices)
+        send_to(put_image.at[peer], got_image.at[me], peer, send_sem.at[4], recv_sem.at[4])
+        return carry
+
+    lax.fori_loop(1, devices, scatter, 0)
+    got_image[me] = put_image[me]
+    wait_all(got_image, devices - 1, recv_sem.at[4])
+    mine[...] = jnp.sum(got_image[...], axis=0)
+
+    def share(k, carry):
+        peer = lax.rem(me + k, devices)
+        send_to(mine, spread.at[me], peer, send_sem.at[5], recv_sem.at[5])
+        return carry
+
+    lax.fori_loop(1, devices, share, 0)
+    spread[me] = mine[...]
+    wait_all(spread, devices - 1, recv_sem.at[5])
+    image = jnp.concatenate([
+        jnp.concatenate([spread[r * spans + k, j] for k in range(spans) for j in range(each)], axis=1)
+        for r in range(high_tiles)], axis=0)
+
+    deal(left_split(image, hat_high[...], hat_low[...]), puts.at[2])
+    exchange(2)
+    inverse = inverse_factor(dot(image, image, ((1,), (1,))))
+    arrive(2)
+    lay(contract(2, left), 3)
+    exchange(3)
+    basis_ref[...] = dot(inverse, image, ((1,), (0,)))
+    arrive(3)
+    core = dot(collect(gots.at[3]), inverse, ((0,), (1,)))
+    for c in range(local_three):
+        for b in range(local_two):
+            core_ref[b, c] = core[(c * local_two + b) * rank_four:(c * local_two + b + 1) * rank_four, :]
+
+    for stage in range(4):
+        wait_all(puts.at[stage], (devices - 1) * tile, send_sem.at[stage])
+    wait_all(put_image, devices - 1, send_sem.at[4])
+    wait_all(spread, devices - 1, send_sem.at[5])
+    wait_all(twos, rows - 1, axis_sem.at[0])
+    wait_all(threes, cols - 1, axis_sem.at[2])
+
+
+def fits(tensor, factor_two, factor_three, factor_four, factor_init):
+    rows, cols = lax.axis_size("row"), lax.axis_size("col")
+    devices = rows * cols
+    first_len, local_two, width = tensor.shape
+    fourth_len, rank_four = factor_four.shape
+    rank_one = factor_init.shape[1]
+    local_three = width // fourth_len
+    same = factor_two.shape[1] == local_two * rows and factor_three.shape[1] == local_three * cols
+    even = rank_one % (8 * devices // local_three) == 0 and rank_one % devices == 0 and local_three * (rank_one // devices) == 8
+    flat = local_two * rank_four == LANES and width == LANES and first_len % LANES == 0
+    tiles = (rank_one // 8) * (first_len // LANES)
+    return same and even and flat and tiles % devices == 0 and (first_len // LANES) % max(tiles // devices, 1) == 0
+
+
+def fused(tensor, factor_two, factor_three, factor_four, factor_init):
+    rows, cols = lax.axis_size("row"), lax.axis_size("col")
+    devices = rows * cols
+    first_len, local_two, width = tensor.shape
+    fourth_len, rank_four = factor_four.shape
+    rank_one = factor_init.shape[1]
+    local_three = width // fourth_len
+    features = local_two * local_three * rank_four
+    total_width = local_two * width
+    tile = local_three * (rank_one // devices)
+    lanes = local_two * rank_four
+    each = (rank_one // 8) * (first_len // LANES) // devices
+    wide = rows * lanes
+    f32, bf16 = jnp.float32, jnp.bfloat16
+    vmem = pl.BlockSpec(memory_space=pltpu.VMEM)
+    core, basis = pl.pallas_call(
+        functools.partial(hooi_kernel, devices),
+        out_shape=(
+            jax.ShapeDtypeStruct((local_two, local_three, rank_four, rank_one), f32),
+            jax.ShapeDtypeStruct((rank_one, first_len), f32),
+        ),
+        in_specs=[pl.BlockSpec(memory_space=pl.ANY), vmem, vmem, vmem, vmem],
+        out_specs=(vmem, vmem),
+        scratch_shapes=[
+            pltpu.VMEM((local_two, first_len, width), f32),
+            pltpu.VMEM((first_len, total_width), bf16),
+            pltpu.VMEM((first_len, total_width), bf16),
+            pltpu.VMEM((total_width, features), bf16),
+            pltpu.VMEM((total_width, features), bf16),
+            pltpu.VMEM((first_len, features), bf16),
+            pltpu.VMEM((first_len, features), bf16),
+            pltpu.VMEM((features, first_len), bf16),
+            pltpu.VMEM((features, first_len), bf16),
+            pltpu.VMEM((wide, wide), bf16),
+            pltpu.VMEM((wide, wide), bf16),
+            pltpu.VMEM((rows,) + factor_two.shape, f32),
+            pltpu.VMEM((cols,) + factor_three.shape, f32),
+            pltpu.VMEM((4, devices * tile, lanes), f32),
+            pltpu.VMEM((4, devices * tile, lanes), f32),
+            pltpu.VMEM((devices, each, 8, LANES), f32),
+            pltpu.VMEM((devices, each, 8, LANES), f32),
+            pltpu.VMEM((each, 8, LANES), f32),
+            pltpu.VMEM((devices, each, 8, LANES), f32),
+            pltpu.SemaphoreType.DMA((local_two,)),
+            pltpu.SemaphoreType.DMA((6,)),
+            pltpu.SemaphoreType.DMA((6,)),
+            pltpu.SemaphoreType.DMA((4,)),
+        ],
+        compiler_params=pltpu.CompilerParams(collective_id=0, has_side_effects=True),
+    )(tensor, factor_two, factor_three, factor_four.T, factor_init.T)
+    return basis.T, core.transpose(3, 0, 1, 2)
+
+
 def shards(tensor, factor_two, factor_three, factor_four, factor_init):
+    if fits(tensor, factor_two, factor_three, factor_four, factor_init):
+        return fused(tensor, factor_two, factor_three, factor_four, factor_init)
     axes = ("row", "col")
     first_len, local_two, width = tensor.shape
     fourth_len, rank_four = factor_four.shape

time: 119 us -> 54.8 us (0.46)
  Pallas kernels: 72.9 us -> 50.6 us
  matrix products: 21.3 us -> 0 us
  local copies, waits for them, and re-layouts: 22.1 us -> 3.34 us
    pallas_call x6 -> x1, Pallas kernels: 72.9 us -> 50.6 us  [fused(): pl.pallas_call(functools.partial(hooi_kernel, devices), out_shape=(jax.Sh...]
    dot_general x11 -> x0, matrix products: 13.3 us -> none  [the longest x1 4.73 us: shards(): jnp.dot(tensor.reshape(first_len, -1), block.reshape(-1, rank_one), preci...]
    unnamed x2 -> x0, matrix products: 8 us -> none
    reshape x11 -> x0, local copies, waits for them, and re-layouts: 5.65 us -> none  [the longest x4 3.39 us: share(): jnp.pad(values, ((0, 0), (0, padded - length)))]
    unnamed x9 -> x2, local copies, waits for them, and re-layouts: 8.38 us -> 3.34 us
    another operation x11 -> x0, local copies, waits for them, and re-layouts: 4.31 us -> none  [the longest x2 2.13 us: gather(): share(put.reshape(devices, -1), ident)]
    slice x5 -> x0, local copies, waits for them, and re-layouts: 1.21 us -> none  [the longest x1 1.15 us: shards(): image = jnp.concatenate([image[:, :rank_one], image[:, rank_one:]], axis=0)]
where the time goes in v1:
time: 54.8 us; the launch traced here: 54.6 us
  Pallas kernels  50.6 us (92%)
  local copies, waits for them, and re-layouts  3.34 us (6%)
  between operations  0.64 us (1%)
    pallas_call x1, Pallas kernels, fused(): pl.pallas_call(functools.partial(hooi_kernel, devices), out_shape=(jax.Sh...  50.6 us
    unnamed x2, local copies, waits for them, and re-layouts  3.34 us

profile of v1, /device:TPU:0, one launch (start us, length us, event | category | flops | bytes accessed | tf_op | source)
XLA Modules:
  0.0 54.6 jit_solution(10397511375891582381)
XLA Ops:
  0.6 50.6 %shard_map.68 = (f32[8,4,16,64]{3,2,1,0:T(8,128)}, f32[64,1024]{1,0:T(8,128)}) custom-call(f32[1024,8,128]{2,1,0:T(8,128)} %tensor_ref.1, f32[8,32]{1,0:T(8,128)} %two_ref.1, f32[4,32]{1,0:T(4,128)} %three_ref.1, f32[16,32]{1,0:T(8,128)} %bitcast.7, f32[64,1024]{1,0:T(8,128)} %bitcast.4), custom_call_target="tpu_custom_call" | custom-call | tf_op jit(solution)/shard_map/pallas_call | solution.py:430
  51.3 1.7 %copy.9 = f32[1024,64]{0,1:T(8,128)} copy(f32[1024,64]{0,1:T(8,128)} %bitcast.6) | data formatting | bytes 524288
  52.9 1.7 %copy.10 = f32[64,8,4,16]{0,3,2,1:T(8,128)} copy(f32[64,8,4,16]{0,3,2,1:T(8,128)} %bitcast.5) | data formatting | bytes 262144

commit v2 on v0

--- a/solution.py
+++ b/solution.py
@@ -139,7 +139,430 @@
     )(values)
 
 
+def split(x):
+    high = x.astype(jnp.bfloat16)
+    return high, (x - high.astype(jnp.float32)).astype(jnp.bfloat16)
+
+
+def narrow(a, b):
+    return lax.dot_general(a, b, (((1,), (0,)), ((), ())), preferred_element_type=jnp.float32)
+
+
+def left_split(x, high, low):
+    rows = x.shape[0]
+    top, rest = split(x)
+    both = narrow(jnp.concatenate([top, rest], axis=0), high)
+    return both[:rows] + both[rows:] + narrow(top, low)
+
+
+def iota(shape, dim):
+    return lax.broadcasted_iota(jnp.int32, shape, dim)
+
+
+def ones_where(mask):
+    return jnp.where(mask, 1.0, 0.0).astype(jnp.float32)
+
+
+def expand_rows(square, copies):
+    tall = (square.shape[0] * copies, square.shape[0])
+    wide = (square.shape[1], square.shape[1] * copies)
+    result = dot(ones_where(iota(tall, 0) // copies == iota(tall, 1)), square, ((1,), (0,)))
+    result = dot(result, ones_where(iota(wide, 1) // copies == iota(wide, 0)), ((1,), (0,)))
+    return jnp.where(iota(result.shape, 0) % copies == iota(result.shape, 1) % copies, result, 0.0)
+
+
+def store_lanes(matrix, copies, high_ref, low_ref):
+    shape = (matrix.shape[1], matrix.shape[1] * copies)
+    wide = dot(matrix, ones_where(iota(shape, 1) // copies == iota(shape, 0)), ((1,), (0,)))
+    shape = (copies, shape[1])
+    keep = iota(shape, 1) % copies == iota(shape, 0)
+    for k in range(matrix.shape[0]):
+        high, low = split(jnp.where(keep, jnp.broadcast_to(wide[k:k + 1, :], shape), 0.0))
+        high_ref[k * copies:(k + 1) * copies, :] = high
+        low_ref[k * copies:(k + 1) * copies, :] = low
+
+
+def eliminate(left, right, first, last):
+    size = left.shape[0]
+    index = iota((size, 1), 0)
+    for k in range(first, last):
+        scale = lax.rsqrt(left[k:k + 1, k:k + 1])
+        column = left[:, k:k + 1] * scale
+        pivot_left = left[k:k + 1, :] * scale
+        pivot_right = right[k:k + 1, :] * scale
+        factor = jnp.where(index > k, column, 0.0)
+        left = left - factor * pivot_left
+        right = jnp.where(index == k, pivot_right, right - factor * pivot_right)
+    return left, right
+
+
+def copy_to(source, target, row, col, send_sem, recv_sem):
+    pltpu.make_async_remote_copy(
+        src_ref=source,
+        dst_ref=target,
+        send_sem=send_sem,
+        recv_sem=recv_sem,
+        device_id=(row, col),
+        device_id_type=pl.DeviceIdType.MESH,
+    ).start()
+
+
+def wait_for(ref, sem):
+    pltpu.make_async_copy(ref, ref, sem).wait()
+
+
+def hooi_kernel(tensor_hbm, two_hbm, three_hbm, four_hbm, init_hbm, core_ref, basis_ref,
+                slabs, two_ref, three_ref, four_ref, init_ref,
+                high_ref, low_ref, mix_high, mix_low, hat_high, hat_low, turn_high, turn_low,
+                lane_high, lane_low, twos, threes, deals, dealt, backs, backed,
+                parts, paired, sums, shares, mine, spread,
+                load_sem, factor_sem, send_sem, deal_sem, back_sem, image_sem):
+    rows, cols = lax.axis_size("row"), lax.axis_size("col")
+    row, col = lax.axis_index("row"), lax.axis_index("col")
+    devices = rows * cols
+    members = devices // 2
+    half = lax.rem(row, 2)
+    seat = (row // 2) * cols + col
+    me = row * cols + col
+    partner = row + 1 - 2 * half
+    rank_one, first_len = init_ref.shape
+    half_rank = rank_one // 2
+    local_two, local_three = two_ref.shape[0], three_ref.shape[0]
+    rank_four, fourth_len = four_ref.shape
+    width = local_three * fourth_len
+    lanes = local_two * rank_four
+    features = local_three * lanes
+    copies = rank_one // devices
+    tile = local_three * copies
+    each = sums.shape[2]
+
+    slab_loads = [pltpu.make_async_copy(tensor_hbm.at[:, b, :], slabs.at[b], load_sem.at[b]) for b in range(local_two)]
+    small = [(four_hbm, four_ref), (init_hbm, init_ref), (two_hbm, two_ref), (three_hbm, three_ref)]
+    small_loads = [pltpu.make_async_copy(source, target, load_sem.at[local_two + k]) for k, (source, target) in enumerate(small)]
+    small_loads[0].start()
+    small_loads[1].start()
+    for load in slab_loads:
+        load.start()
+    small_loads[2].start()
+    small_loads[3].start()
+
+    barrier = pltpu.get_barrier_semaphore()
+
+    def hello(k, carry):
+        peer = lax.rem(me + k, devices)
+        pl.semaphore_signal(barrier, inc=1, device_id=(peer // cols, lax.rem(peer, cols)), device_id_type=pl.DeviceIdType.MESH)
+        return carry
+
+    lax.fori_loop(1, devices, hello, 0)
+
+    def target(k):
+        turn = k // (rows // 2)
+        shift = (turn + 1) // 2
+        there = lax.rem(col + cols // 2 + cols + (1 - 2 * lax.rem(turn, 2)) * shift, cols)
+        return lax.rem(row // 2 + rows - 1 - lax.rem(k, rows // 2), rows // 2), there
+
+    def at(index, count):
+        return pl.ds(pl.multiple_of(index * count, count), count)
+
+    small_loads[0].wait()
+    lane = iota((fourth_len, features), 1)
+    shape = (rank_four, features)
+    four = dot(four_ref[...], ones_where(iota(shape, 1) % rank_four == iota(shape, 0)), ((0,), (0,)))
+    four_high = four.astype(jnp.bfloat16).astype(jnp.float32)
+    four_low = four - four_high
+    for b in range(local_two):
+        for c in range(local_three):
+            keep = lane // rank_four == c * local_two + b
+            part = slice((b * local_three + c) * fourth_len, (b * local_three + c + 1) * fourth_len)
+            mix_high[part, :] = jnp.where(keep, four_high, 0.0).astype(jnp.bfloat16)
+            mix_low[part, :] = jnp.where(keep, four_low, 0.0).astype(jnp.bfloat16)
+
+    small_loads[1].wait()
+    init_high, init_low = split(init_ref[...])
+    init_both = jnp.concatenate([init_high, init_low], axis=0)
+    group = 2 if local_two % 2 == 0 else 1
+
+    def pull_group(b):
+        part = slice(b * width, (b + group) * width)
+        both = narrow(init_both, high_ref[:, part])
+        pulled = both[:rank_one] + both[rank_one:] + narrow(init_high, low_ref[:, part])
+        return left_split(pulled, mix_high[part, :], mix_low[part, :])
+
+    vectors = None
+    for b in range(0, local_two, group):
+        for k in range(b, b + group):
+            slab_loads[k].wait()
+            high, low = split(slabs[k])
+            high_ref[:, k * width:(k + 1) * width] = high
+            low_ref[:, k * width:(k + 1) * width] = low
+        if b > 0:
+            more = pull_group(b - group)
+            vectors = more if vectors is None else vectors + more
+    more = pull_group(local_two - group)
+    vectors = more if vectors is None else vectors + more
+
+    def deal(vectors, put):
+        for c in range(local_three):
+            for k in range(copies):
+                put[pl.ds(c * copies + k, members, stride=tile), :] = vectors[k * members:(k + 1) * members, c * lanes:(c + 1) * lanes]
+
+    def send_deal(stage, h):
+        def send(k, carry):
+            there_row, there_col = target(k)
+            copy_to(deals.at[stage, h, at(there_row * cols + there_col, tile)], dealt.at[stage, at(me, tile)],
+                    there_row * 2 + h, there_col, send_sem.at[stage], deal_sem.at[stage])
+            return carry
+
+        lax.fori_loop(0, members - jnp.where(half == h, 1, 0), send, 0)
+
+    def wait_deal(stage):
+        dealt[stage, at(me, tile), :] = deals[stage, half, at(seat, tile), :]
+        wait_for(dealt.at[stage, pl.ds(0, (devices - 1) * tile)], deal_sem.at[stage])
+
+    def contract(stage, matrix):
+        high, low = split(matrix)
+        size = matrix.shape[0]
+        block = jnp.concatenate([dealt[stage, k * cols * tile:(k + 1) * cols * tile, :] for k in range(rows)], axis=1)
+        top, rest = split(block)
+        mixed = narrow(jnp.concatenate([high, low], axis=0), top)
+        mixed = mixed[:size] + mixed[size:] + narrow(high, rest)
+        result = left_split(mixed, lane_high[...], lane_low[...])
+        for k in range(rows):
+            backs[stage, k * cols * tile:(k + 1) * cols * tile, :] = result[:, k * lanes:(k + 1) * lanes]
+
+    def send_back(stage):
+        def send(k, carry):
+            there_row, there_col = target(k)
+            for h in range(2):
+                copy_to(backs.at[stage, at((there_row * 2 + h) * cols + there_col, tile)], backed.at[stage, half, at(seat, tile)],
+                        there_row * 2 + h, there_col, send_sem.at[2 + stage], back_sem.at[stage, half])
+            return carry
+
+        lax.fori_loop(0, members - 1, send, 0)
+        copy_to(backs.at[stage, at(partner * cols + col, tile)], backed.at[stage, half, at(seat, tile)],
+                partner, col, send_sem.at[2 + stage], back_sem.at[stage, half])
+        backed[stage, half, at(seat, tile), :] = backs[stage, at(me, tile), :]
+
+    def wait_back(stage, h):
+        @pl.when(half == h)
+        def _():
+            wait_for(backed.at[stage, h, pl.ds(0, (members - 1) * tile)], back_sem.at[stage, h])
+
+        @pl.when(half != h)
+        def _():
+            wait_for(backed.at[stage, h], back_sem.at[stage, h])
+
+    def collect(stage, h):
+        return jnp.concatenate([
+            jnp.concatenate([backed[stage, h, pl.ds(c * copies + k, members, stride=tile), :] for k in range(copies)], axis=0)
+            for c in range(local_three)], axis=1)
+
+    for h in range(2):
+        deal(vectors[h * half_rank:(h + 1) * half_rank], deals.at[0, h])
+    small_loads[2].wait()
+    small_loads[3].wait()
+    pl.semaphore_wait(barrier, devices - 1)
+
+    send_deal(0, 0)
+    send_deal(0, 1)
+
+    def send_two(k, carry):
+        copy_to(two_ref, twos.at[row], lax.rem(row + k, rows), col, factor_sem.at[0], factor_sem.at[1])
+        return carry
+
+    def send_three(k, carry):
+        copy_to(three_ref, threes.at[col], row, lax.rem(col + k, cols), factor_sem.at[2], factor_sem.at[3])
+        return carry
+
+    lax.fori_loop(1, rows, send_two, 0)
+    lax.fori_loop(1, cols, send_three, 0)
+    twos[row] = two_ref[...]
+    threes[col] = three_ref[...]
+
+    def hat_piece(k, count):
+        part = slice(k * first_len // count, (k + 1) * first_len // count)
+        hat = narrow(high_ref[part, :], mix_high[...]) + narrow(high_ref[part, :], mix_low[...]) + narrow(low_ref[part, :], mix_high[...])
+        hat_high[part, :], hat_low[part, :] = split(hat)
+        turn_high[:, part], turn_low[:, part] = split(hat.T)
+
+    hat_piece(0, 4)
+    hat_piece(1, 4)
+    wait_for(twos.at[pl.ds(0, rows - 1)], factor_sem.at[1])
+    wait_for(threes.at[pl.ds(0, cols - 1)], factor_sem.at[3])
+    whole_two = jnp.concatenate([twos[k] for k in range(rows)], axis=0)
+    whole_three = jnp.concatenate([threes[k] for k in range(cols)], axis=0)
+    store_lanes(dot(whole_two, whole_two, ((1,), (1,))), rank_four, lane_high, lane_low)
+    left = expand_rows(dot(whole_three, whole_three, ((1,), (1,))), copies)
+
+    wait_deal(0)
+    contract(0, left)
+    send_back(0)
+    hat_piece(2, 4)
+    hat_piece(3, 4)
+
+    spans = first_len // LANES // each
+    for h in range(2):
+        wait_back(0, h)
+        image = left_split(collect(0, h), turn_high[...], turn_low[...])
+        for i in range(devices):
+            for j in range(each):
+                r, w = i // spans, (i % spans) * each + j
+                parts[h, i // members, i % members, j] = image[r * 8:(r + 1) * 8, w * LANES:(w + 1) * LANES]
+        copy_to(parts.at[h, 1 - half], paired.at[h], partner, col, image_sem.at[0, h], image_sem.at[1, h])
+
+    for h in range(2):
+        wait_for(paired.at[h], image_sem.at[1, h])
+        sums[h] = parts[h, half] + paired[h]
+
+        def scatter(k, carry):
+            there_row, there_col = target(k)
+            copy_to(sums.at[h, there_row * cols + there_col], shares.at[h, seat], there_row * 2 + half, there_col, image_sem.at[2, h], image_sem.at[3, h])
+            return carry
+
+        lax.fori_loop(0, members - 1, scatter, 0)
+        shares[h, seat] = sums[h, seat]
+
+    for h in range(2):
+        wait_for(shares.at[h, pl.ds(0, members - 1)], image_sem.at[3, h])
+        mine[h] = jnp.sum(shares[h], axis=0)
+
+        def gather(k, carry):
+            there_row, there_col = target(k)
+            copy_to(mine.at[h], spread.at[h, half, seat], there_row * 2 + half, there_col, image_sem.at[4, h], image_sem.at[5, h])
+            return carry
+
+        lax.fori_loop(0, members - 1, gather, 0)
+        spread[h, half, seat] = mine[h]
+
+    for h in range(2):
+        wait_for(spread.at[h, half, pl.ds(0, members - 1)], image_sem.at[5, h])
+        copy_to(spread.at[h, half], spread.at[h, half], partner, col, image_sem.at[6, h], image_sem.at[7, h])
+
+    images = []
+    for h in range(2):
+        wait_for(spread.at[h, half], image_sem.at[7, h])
+        images.append(jnp.concatenate([
+            jnp.concatenate([spread[h, i // members, i % members, j] for i in range(r * spans, (r + 1) * spans) for j in range(each)], axis=1)
+            for r in range(half_rank // 8)], axis=0))
+        deal(left_split(images[h], hat_high[...], hat_low[...]), deals.at[1, h])
+        send_deal(1, h)
+
+    image = jnp.concatenate(images, axis=0)
+    lower = dot(image, image, ((1,), (1,)))
+    shape = lower.shape
+    lower, inverse = eliminate(lower, ones_where(iota(shape, 0) == iota(shape, 1)), 0, rank_one // 3)
+    store_lanes(whole_two, rank_four, lane_high, lane_low)
+    left = expand_rows(whole_three.T, copies)
+    wait_deal(1)
+    contract(1, left)
+    send_back(1)
+    lower, inverse = eliminate(lower, inverse, rank_one // 3, rank_one)
+    basis_ref[...] = dot(inverse, image, ((1,), (0,)))
+    wait_back(1, 0)
+    wait_back(1, 1)
+    core = dot(jnp.concatenate([collect(1, 0), collect(1, 1)], axis=0), inverse, ((0,), (1,)))
+    for c in range(local_three):
+        for b in range(local_two):
+            core_ref[b, c] = core[(c * local_two + b) * rank_four:(c * local_two + b + 1) * rank_four, :]
+
+    for stage in range(2):
+        wait_for(dealt.at[stage, pl.ds(0, (devices - 1) * tile)], send_sem.at[stage])
+        wait_for(dealt.at[stage, pl.ds(0, (devices - 1) * tile)], send_sem.at[2 + stage])
+    for h in range(2):
+        wait_for(paired.at[h], image_sem.at[0, h])
+        wait_for(shares.at[h, pl.ds(0, members - 1)], image_sem.at[2, h])
+        wait_for(shares.at[h, pl.ds(0, members - 1)], image_sem.at[4, h])
+        wait_for(paired.at[h], image_sem.at[6, h])
+    wait_for(twos.at[pl.ds(0, rows - 1)], factor_sem.at[0])
+    wait_for(threes.at[pl.ds(0, cols - 1)], factor_sem.at[2])
+
+
+def write_kernel(core_ref, basis_ref, core_hbm, basis_hbm, sem):
+    first = pltpu.make_async_copy(core_ref, core_hbm, sem.at[0])
+    second = pltpu.make_async_copy(basis_ref, basis_hbm, sem.at[1])
+    first.start()
+    second.start()
+    first.wait()
+    second.wait()
+
+
+def fits(tensor, factor_two, factor_three, factor_four, factor_init):
+    rows, cols = lax.axis_size("row"), lax.axis_size("col")
+    devices = rows * cols
+    first_len, local_two, width = tensor.shape
+    fourth_len, rank_four = factor_four.shape
+    rank_one = factor_init.shape[1]
+    local_three = width // fourth_len
+    same = factor_two.shape[1] == local_two * rows and factor_three.shape[1] == local_three * cols
+    even = rows % 2 == 0 and cols % 2 == 0 and rank_one % 16 == 0 and rank_one % devices == 0
+    flat = local_two * rank_four == LANES and width == LANES and local_three * (rank_one // devices) == 8
+    tiles = (rank_one // 16) * (first_len // LANES)
+    return same and even and flat and first_len % (4 * LANES) == 0 and tiles % devices == 0 and (first_len // LANES) % (tiles // devices) == 0
+
+
+def fused(tensor, factor_two, factor_three, factor_four, factor_init):
+    rows, cols = lax.axis_size("row"), lax.axis_size("col")
+    devices = rows * cols
+    members = devices // 2
+    first_len, local_two, width = tensor.shape
+    fourth_len, rank_four = factor_four.shape
+    rank_one = factor_init.shape[1]
+    local_three = width // fourth_len
+    lanes = local_two * rank_four
+    features = local_three * lanes
+    total_width = local_two * width
+    tile = local_three * (rank_one // devices)
+    each = (rank_one // 16) * (first_len // LANES) // devices
+    wide = rows * lanes
+
+    def f32(*shape):
+        return pltpu.VMEM(shape, jnp.float32)
+
+    def bf16(*shape):
+        return pltpu.VMEM(shape, jnp.bfloat16)
+
+    vmem, hbm = pl.BlockSpec(memory_space=pltpu.VMEM), pl.BlockSpec(memory_space=pltpu.HBM)
+    shapes = (
+        jax.ShapeDtypeStruct((local_two, local_three, rank_four, rank_one), jnp.float32),
+        jax.ShapeDtypeStruct((rank_one, first_len), jnp.float32),
+    )
+    operands = [pltpu.with_memory_space_constraint(x, pltpu.HBM) for x in (tensor, factor_two, factor_three, factor_four.T, factor_init.T)]
+    core, basis = pl.pallas_call(
+        hooi_kernel,
+        out_shape=tuple(pltpu.VMEM(x.shape, x.dtype) for x in shapes),
+        in_specs=[hbm] * 5,
+        out_specs=(vmem, vmem),
+        scratch_shapes=[
+            f32(local_two, first_len, width), f32(*factor_two.shape), f32(*factor_three.shape), f32(rank_four, fourth_len), f32(rank_one, first_len),
+            bf16(first_len, total_width), bf16(first_len, total_width), bf16(total_width, features), bf16(total_width, features),
+            bf16(first_len, features), bf16(first_len, features), bf16(features, first_len), bf16(features, first_len),
+            bf16(wide, wide), bf16(wide, wide), f32(rows, *factor_two.shape), f32(cols, *factor_three.shape),
+            f32(2, 2, members * tile, lanes), f32(2, devices * tile, lanes), f32(2, devices * tile, lanes), f32(2, 2, members * tile, lanes),
+            f32(2, 2, members, each, 8, LANES), f32(2, members, each, 8, LANES), f32(2, members, each, 8, LANES), f32(2, members, each, 8, LANES),
+            f32(2, each, 8, LANES), f32(2, 2, members, each, 8, LANES),
+            pltpu.SemaphoreType.DMA((local_two + 4,)),
+            pltpu.SemaphoreType.DMA((4,)),
+            pltpu.SemaphoreType.DMA((4,)),
+            pltpu.SemaphoreType.DMA((2,)),
+            pltpu.SemaphoreType.DMA((2, 2)),
+            pltpu.SemaphoreType.DMA((8, 2)),
+        ],
+        compiler_params=pltpu.CompilerParams(collective_id=0, has_side_effects=True, vmem_limit_bytes=48 << 20),
+    )(*operands)
+    core, basis = pl.pallas_call(
+        write_kernel,
+        out_shape=shapes,
+        in_specs=[vmem, vmem],
+        out_specs=(hbm, hbm),
+        scratch_shapes=[pltpu.SemaphoreType.DMA((2,))],
+        compiler_params=pltpu.CompilerParams(vmem_limit_bytes=4 << 20),
+    )(core, basis)
+    return basis.T, core.transpose(3, 0, 1, 2)
+
+
 def shards(tensor, factor_two, factor_three, factor_four, factor_init):
+    if fits(tensor, factor_two, factor_three, factor_four, factor_init):
+        return fused(tensor, factor_two, factor_three, factor_four, factor_init)
     axes = ("row", "col")
     first_len, local_two, width = tensor.shape
     fourth_len, rank_four = factor_four.shape

time: 119 us -> 47.2 us (0.40)
  Pallas kernels: 72.9 us -> 46.3 us
  local copies, waits for them, and re-layouts: 22.1 us -> 0 us
  matrix products: 21.3 us -> 0 us
    pallas_call x6 -> x2, Pallas kernels: 72.9 us -> 46.3 us  [the longest x1 45.5 us: fused(): pl.pallas_call(hooi_kernel, out_shape=tuple((pltpu.VMEM(x.shape, x.dtype)...]
    dot_general x11 -> x0, matrix products: 13.3 us -> none  [the longest x1 4.73 us: shards(): jnp.dot(tensor.reshape(first_len, -1), block.reshape(-1, rank_one), preci...]
    unnamed x9 -> x0, local copies, waits for them, and re-layouts: 8.38 us -> none
    unnamed x2 -> x0, matrix products: 8 us -> none
    reshape x11 -> x0, local copies, waits for them, and re-layouts: 5.65 us -> none  [the longest x4 3.39 us: share(): jnp.pad(values, ((0, 0), (0, padded - length)))]
    another operation x11 -> x0, local copies, waits for them, and re-layouts: 4.31 us -> none  [the longest x2 2.13 us: gather(): share(put.reshape(devices, -1), ident)]
    slice x5 -> x0, local copies, waits for them, and re-layouts: 1.21 us -> none  [the longest x1 1.15 us: shards(): image = jnp.concatenate([image[:, :rank_one], image[:, rank_one:]], axis=0)]
where the time goes in v2:
time: 47.2 us; the launch traced here: 47 us
  Pallas kernels  46.3 us (98%)
  between operations  0.64 us (1%)
    pallas_call x1, Pallas kernels, fused(): pl.pallas_call(hooi_kernel, out_shape=tuple((pltpu.VMEM(x.shape, x.dtype)...  45.5 us

profile of v2, /device:TPU:0, one launch (start us, length us, event | category | flops | bytes accessed | tf_op | source)
XLA Modules:
  0.0 47.0 jit_solution(6680177145784427895)
XLA Ops:
  0.6 45.5 %shard_map.68 = (f32[8,4,16,64]{3,2,1,0:T(8,128)S(1)}, f32[64,1024]{1,0:T(8,128)S(1)}) custom-call(f32[1024,8,128]{2,1,0:T(8,128)} %tensor_hbm.1, f32[8,32]{1,0:T(8,128)} %two_hbm.1, f32[4,32]{1,0:T(4,128)} %three_hbm.1, f32[16,32]{1,0:T(8,128)} %bitcast.5, f32[64,1024]{1,0:T(8,128)} %bitcast.4), custom_call_target="tpu_custom_call" | custom-call | tf_op jit(solution)/shard_map/pallas_call | solution.py:530
  46.2 0.8 %shard_map.69 = (f32[8,4,16,64]{3,2,1,0:T(8,128)}, f32[64,1024]{1,0:T(8,128)}) custom-call(f32[8,4,16,64]{3,2,1,0:T(8,128)S(1)} %get-tuple-element.6.core_ref, f32[64,1024]{1,0:T(8,128)S(1)} %get-tuple-element.7.basis_ref), custom_call_target="tpu_custom_call" | custom-call | tf_op jit(solution)/shard_map/pallas_call | solution.py:552

commit v3 on v2

--- a/solution.py
+++ b/solution.py
@@ -214,9 +214,9 @@
 def hooi_kernel(tensor_hbm, two_hbm, three_hbm, four_hbm, init_hbm, core_ref, basis_ref,
                 slabs, two_ref, three_ref, four_ref, init_ref,
                 high_ref, low_ref, mix_high, mix_low, hat_high, hat_low, turn_high, turn_low,
-                lane_high, lane_low, twos, threes, deals, dealt, backs, backed,
+                lane_high, lane_low, twos, threes, puts, gots,
                 parts, paired, sums, shares, mine, spread,
-                load_sem, factor_sem, send_sem, deal_sem, back_sem, image_sem):
+                load_sem, factor_sem, send_sem, recv_sem, image_sem, share_sem):
     rows, cols = lax.axis_size("row"), lax.axis_size("col")
     row, col = lax.axis_index("row"), lax.axis_index("col")
     devices = rows * cols
@@ -226,7 +226,7 @@
     me = row * cols + col
     partner = row + 1 - 2 * half
     rank_one, first_len = init_ref.shape
-    half_rank = rank_one // 2
+    half_len = first_len // 2
     local_two, local_three = two_ref.shape[0], three_ref.shape[0]
     rank_four, fourth_len = four_ref.shape
     width = local_three * fourth_len
@@ -234,7 +234,8 @@
     features = local_three * lanes
     copies = rank_one // devices
     tile = local_three * copies
-    each = sums.shape[2]
+    each = sums.shape[0]
+    spans = half_len // LANES
 
     slab_loads = [pltpu.make_async_copy(tensor_hbm.at[:, b, :], slabs.at[b], load_sem.at[b]) for b in range(local_two)]
     small = [(four_hbm, four_ref), (init_hbm, init_ref), (two_hbm, two_ref), (three_hbm, three_ref)]
@@ -246,15 +247,6 @@
     small_loads[2].start()
     small_loads[3].start()
 
-    barrier = pltpu.get_barrier_semaphore()
-
-    def hello(k, carry):
-        peer = lax.rem(me + k, devices)
-        pl.semaphore_signal(barrier, inc=1, device_id=(peer // cols, lax.rem(peer, cols)), device_id_type=pl.DeviceIdType.MESH)
-        return carry
-
-    lax.fori_loop(1, devices, hello, 0)
-
     def target(k):
         turn = k // (rows // 2)
         shift = (turn + 1) // 2
@@ -263,6 +255,24 @@
 
     def at(index, count):
         return pl.ds(pl.multiple_of(index * count, count), count)
+
+    barrier = pltpu.get_barrier_semaphore()
+
+    def greet_at(there_row, there_col):
+        pl.semaphore_signal(barrier, inc=1, device_id=(there_row, there_col), device_id_type=pl.DeviceIdType.MESH)
+
+    def hello(k, carry):
+        there_row, there_col = target(members - 1 - rows // 2 - k)
+        greet_at(there_row * 2, there_col)
+        greet_at(there_row * 2 + 1, there_col)
+        return carry
+
+    def hello_near(k, carry):
+        greet_at(lax.rem(row + k, rows), col)
+        return carry
+
+    lax.fori_loop(0, members - rows // 2, hello, 0)
+    lax.fori_loop(1, rows, hello_near, 0)
 
     small_loads[0].wait()
     lane = iota((fourth_len, features), 1)
@@ -280,92 +290,87 @@
     small_loads[1].wait()
     init_high, init_low = split(init_ref[...])
     init_both = jnp.concatenate([init_high, init_low], axis=0)
-    group = 2 if local_two % 2 == 0 else 1
-
-    def pull_group(b):
-        part = slice(b * width, (b + group) * width)
+    group = 4 if local_two % 4 == 0 else 1
+    count = local_two // group
+
+    def pull_group(k):
+        part = slice(k * group * width, (k + 1) * group * width)
         both = narrow(init_both, high_ref[:, part])
-        pulled = both[:rank_one] + both[rank_one:] + narrow(init_high, low_ref[:, part])
+        return both[:rank_one] + both[rank_one:] + narrow(init_high, low_ref[:, part])
+
+    def mix_group(k, pulled):
+        part = slice(k * group * width, (k + 1) * group * width)
         return left_split(pulled, mix_high[part, :], mix_low[part, :])
 
-    vectors = None
-    for b in range(0, local_two, group):
-        for k in range(b, b + group):
-            slab_loads[k].wait()
-            high, low = split(slabs[k])
-            high_ref[:, k * width:(k + 1) * width] = high
-            low_ref[:, k * width:(k + 1) * width] = low
-        if b > 0:
-            more = pull_group(b - group)
-            vectors = more if vectors is None else vectors + more
-    more = pull_group(local_two - group)
-    vectors = more if vectors is None else vectors + more
+    pulled, vectors = [], []
+    for k in range(count + 2):
+        if k < count:
+            for b in range(k * group, (k + 1) * group):
+                slab_loads[b].wait()
+                high, low = split(slabs[b])
+                high_ref[:, b * width:(b + 1) * width] = high
+                low_ref[:, b * width:(b + 1) * width] = low
+        if k >= 2:
+            vectors.append(mix_group(k - 2, pulled[k - 2]))
+        if 1 <= k <= count:
+            pulled.append(pull_group(k - 1))
+    vectors = sum(vectors[1:], vectors[0])
 
     def deal(vectors, put):
         for c in range(local_three):
             for k in range(copies):
-                put[pl.ds(c * copies + k, members, stride=tile), :] = vectors[k * members:(k + 1) * members, c * lanes:(c + 1) * lanes]
-
-    def send_deal(stage, h):
-        def send(k, carry):
+                put[pl.ds(c * copies + k, devices, stride=tile), :] = vectors[k * devices:(k + 1) * devices, c * lanes:(c + 1) * lanes]
+
+    def send(stage):
+        put, got = puts.at[stage], gots.at[stage]
+
+        def one(there_row, there_col):
+            copy_to(put.at[at(there_row * cols + there_col, tile)], got.at[at(me, tile)], there_row, there_col, send_sem.at[stage], recv_sem.at[stage])
+
+        def some(k, carry):
+            there_row, there_col = target(lax.rem(k, members - 1))
+            one(there_row * 2 + k // (members - 1), there_col)
+            return carry
+
+        def both(k, carry):
             there_row, there_col = target(k)
-            copy_to(deals.at[stage, h, at(there_row * cols + there_col, tile)], dealt.at[stage, at(me, tile)],
-                    there_row * 2 + h, there_col, send_sem.at[stage], deal_sem.at[stage])
+            one(there_row * 2, there_col)
+            one(there_row * 2 + 1, there_col)
             return carry
 
-        lax.fori_loop(0, members - jnp.where(half == h, 1, 0), send, 0)
-
-    def wait_deal(stage):
-        dealt[stage, at(me, tile), :] = deals[stage, half, at(seat, tile), :]
-        wait_for(dealt.at[stage, pl.ds(0, (devices - 1) * tile)], deal_sem.at[stage])
+        if stage in (0, 1, 2, 3):
+            lax.fori_loop(0, 2 * (members - 1), some, 0, unroll=5 if (members - 1) % 5 == 0 else 1)
+        else:
+            lax.fori_loop(0, members - 1, both, 0, unroll=3 if (members - 1) % 3 == 0 else 1)
+        one(partner, col)
+        here = at(me, tile)
+        got[here, :] = put[here, :]
+
+    def arrive(stage):
+        wait_for(gots.at[stage, pl.ds(0, (devices - 1) * tile)], recv_sem.at[stage])
 
     def contract(stage, matrix):
+        block = jnp.concatenate([gots[stage, k * cols * tile:(k + 1) * cols * tile, :] for k in range(rows)], axis=1)
+        top, rest = split(block)
+        result = left_split(narrow(matrix, jnp.concatenate([top, top, rest], axis=0)), lane_high[...], lane_low[...])
+        for k in range(rows):
+            puts[stage + 1, k * cols * tile:(k + 1) * cols * tile, :] = result[:, k * lanes:(k + 1) * lanes]
+
+    def triple(matrix, axis):
         high, low = split(matrix)
-        size = matrix.shape[0]
-        block = jnp.concatenate([dealt[stage, k * cols * tile:(k + 1) * cols * tile, :] for k in range(rows)], axis=1)
-        top, rest = split(block)
-        mixed = narrow(jnp.concatenate([high, low], axis=0), top)
-        mixed = mixed[:size] + mixed[size:] + narrow(high, rest)
-        result = left_split(mixed, lane_high[...], lane_low[...])
-        for k in range(rows):
-            backs[stage, k * cols * tile:(k + 1) * cols * tile, :] = result[:, k * lanes:(k + 1) * lanes]
-
-    def send_back(stage):
-        def send(k, carry):
-            there_row, there_col = target(k)
-            for h in range(2):
-                copy_to(backs.at[stage, at((there_row * 2 + h) * cols + there_col, tile)], backed.at[stage, half, at(seat, tile)],
-                        there_row * 2 + h, there_col, send_sem.at[2 + stage], back_sem.at[stage, half])
-            return carry
-
-        lax.fori_loop(0, members - 1, send, 0)
-        copy_to(backs.at[stage, at(partner * cols + col, tile)], backed.at[stage, half, at(seat, tile)],
-                partner, col, send_sem.at[2 + stage], back_sem.at[stage, half])
-        backed[stage, half, at(seat, tile), :] = backs[stage, at(me, tile), :]
-
-    def wait_back(stage, h):
-        @pl.when(half == h)
-        def _():
-            wait_for(backed.at[stage, h, pl.ds(0, (members - 1) * tile)], back_sem.at[stage, h])
-
-        @pl.when(half != h)
-        def _():
-            wait_for(backed.at[stage, h], back_sem.at[stage, h])
-
-    def collect(stage, h):
+        return jnp.concatenate([high, low, high], axis=axis)
+
+    def collect(stage):
+        got = gots.at[stage]
         return jnp.concatenate([
-            jnp.concatenate([backed[stage, h, pl.ds(c * copies + k, members, stride=tile), :] for k in range(copies)], axis=0)
+            jnp.concatenate([got[pl.ds(c * copies + k, devices, stride=tile), :] for k in range(copies)], axis=0)
             for c in range(local_three)], axis=1)
 
-    for h in range(2):
-        deal(vectors[h * half_rank:(h + 1) * half_rank], deals.at[0, h])
+    deal(vectors, puts.at[0])
     small_loads[2].wait()
     small_loads[3].wait()
     pl.semaphore_wait(barrier, devices - 1)
 
-    send_deal(0, 0)
-    send_deal(0, 1)
-
     def send_two(k, carry):
         copy_to(two_ref, twos.at[row], lax.rem(row + k, rows), col, factor_sem.at[0], factor_sem.at[1])
         return carry
@@ -376,6 +381,7 @@
 
     lax.fori_loop(1, rows, send_two, 0)
     lax.fori_loop(1, cols, send_three, 0)
+    send(0)
     twos[row] = two_ref[...]
     threes[col] = three_ref[...]
 
@@ -392,87 +398,97 @@
     whole_two = jnp.concatenate([twos[k] for k in range(rows)], axis=0)
     whole_three = jnp.concatenate([threes[k] for k in range(cols)], axis=0)
     store_lanes(dot(whole_two, whole_two, ((1,), (1,))), rank_four, lane_high, lane_low)
-    left = expand_rows(dot(whole_three, whole_three, ((1,), (1,))), copies)
-
-    wait_deal(0)
+    left = triple(expand_rows(dot(whole_three, whole_three, ((1,), (1,))), copies), 1)
+
+    arrive(0)
     contract(0, left)
-    send_back(0)
+    send(1)
     hat_piece(2, 4)
     hat_piece(3, 4)
 
-    spans = first_len // LANES // each
-    for h in range(2):
-        wait_back(0, h)
-        image = left_split(collect(0, h), turn_high[...], turn_low[...])
-        for i in range(devices):
+    arrive(1)
+    back = collect(1)
+
+    def image_part(which):
+        span = at(which, half_len)
+        return left_split(back, turn_high[:, span], turn_low[:, span])
+
+    def tiles():
+        for i in range(members):
             for j in range(each):
-                r, w = i // spans, (i % spans) * each + j
-                parts[h, i // members, i % members, j] = image[r * 8:(r + 1) * 8, w * LANES:(w + 1) * LANES]
-        copy_to(parts.at[h, 1 - half], paired.at[h], partner, col, image_sem.at[0, h], image_sem.at[1, h])
-
-    for h in range(2):
-        wait_for(paired.at[h], image_sem.at[1, h])
-        sums[h] = parts[h, half] + paired[h]
-
+                r, w = (i * each + j) // spans, (i * each + j) % spans
+                yield i, j, slice(r * 8, (r + 1) * 8), slice(w * LANES, (w + 1) * LANES)
+
+    image = image_part(1 - half)
+    for i, j, r, w in tiles():
+        parts[j, i] = image[r, w]
+    copy_to(parts, paired, partner, col, image_sem.at[0], image_sem.at[1])
+    image = image_part(half)
+    wait_for(paired, image_sem.at[1])
+    for i, j, r, w in tiles():
+        sums[j, i] = image[r, w] + paired[j, i]
+
+    for j in range(each):
         def scatter(k, carry):
             there_row, there_col = target(k)
-            copy_to(sums.at[h, there_row * cols + there_col], shares.at[h, seat], there_row * 2 + half, there_col, image_sem.at[2, h], image_sem.at[3, h])
+            copy_to(sums.at[j, there_row * cols + there_col], shares.at[j, seat], there_row * 2 + 1 - half, there_col, share_sem.at[0, j], share_sem.at[1, j])
             return carry
 
-        lax.fori_loop(0, members - 1, scatter, 0)
-        shares[h, seat] = sums[h, seat]
-
-    for h in range(2):
-        wait_for(shares.at[h, pl.ds(0, members - 1)], image_sem.at[3, h])
-        mine[h] = jnp.sum(shares[h], axis=0)
+        lax.fori_loop(0, members, scatter, 0, unroll=4)
+    for j in range(each):
+        wait_for(shares.at[j], share_sem.at[1, j])
+        mine[j] = jnp.sum(shares[j], axis=0)
 
         def gather(k, carry):
             there_row, there_col = target(k)
-            copy_to(mine.at[h], spread.at[h, half, seat], there_row * 2 + half, there_col, image_sem.at[4, h], image_sem.at[5, h])
+            copy_to(mine.at[j], spread.at[1 - half, j, seat], there_row * 2 + 1 - half, there_col, share_sem.at[2, j], share_sem.at[3, j])
             return carry
 
-        lax.fori_loop(0, members - 1, gather, 0)
-        spread[h, half, seat] = mine[h]
-
-    for h in range(2):
-        wait_for(spread.at[h, half, pl.ds(0, members - 1)], image_sem.at[5, h])
-        copy_to(spread.at[h, half], spread.at[h, half], partner, col, image_sem.at[6, h], image_sem.at[7, h])
-
-    images = []
-    for h in range(2):
-        wait_for(spread.at[h, half], image_sem.at[7, h])
-        images.append(jnp.concatenate([
-            jnp.concatenate([spread[h, i // members, i % members, j] for i in range(r * spans, (r + 1) * spans) for j in range(each)], axis=1)
-            for r in range(half_rank // 8)], axis=0))
-        deal(left_split(images[h], hat_high[...], hat_low[...]), deals.at[1, h])
-        send_deal(1, h)
-
-    image = jnp.concatenate(images, axis=0)
+        lax.fori_loop(0, members, gather, 0, unroll=4)
+    for j in range(each):
+        wait_for(spread.at[half, j], share_sem.at[3, j])
+        copy_to(spread.at[half, j], spread.at[half, j], partner, col, image_sem.at[2], image_sem.at[3])
+
+    def image_half(which):
+        return jnp.concatenate([
+            jnp.concatenate([spread[which, (r * spans + w) % each, (r * spans + w) // each] for w in range(spans)], axis=1)
+            for r in range(rank_one // 8)], axis=0)
+
+    def pull_half(which):
+        span = at(which, half_len)
+        return left_split(image_half(which), hat_high[span, :], hat_low[span, :])
+
+    vectors = pull_half(half)
+    wait_for(spread.at[1 - half], image_sem.at[3])
+    deal(vectors + pull_half(1 - half), puts.at[2])
+    send(2)
+
+    image = jnp.concatenate([image_half(0), image_half(1)], axis=1)
     lower = dot(image, image, ((1,), (1,)))
     shape = lower.shape
-    lower, inverse = eliminate(lower, ones_where(iota(shape, 0) == iota(shape, 1)), 0, rank_one // 3)
+    lower, inverse = eliminate(lower, ones_where(iota(shape, 0) == iota(shape, 1)), 0, rank_one * 5 // 8)
     store_lanes(whole_two, rank_four, lane_high, lane_low)
-    left = expand_rows(whole_three.T, copies)
-    wait_deal(1)
-    contract(1, left)
-    send_back(1)
-    lower, inverse = eliminate(lower, inverse, rank_one // 3, rank_one)
+    left = triple(expand_rows(whole_three.T, copies), 1)
+    arrive(2)
+    contract(2, left)
+    send(3)
+    lower, inverse = eliminate(lower, inverse, rank_one * 5 // 8, rank_one)
     basis_ref[...] = dot(inverse, image, ((1,), (0,)))
-    wait_back(1, 0)
-    wait_back(1, 1)
-    core = dot(jnp.concatenate([collect(1, 0), collect(1, 1)], axis=0), inverse, ((0,), (1,)))
+    inverse_high, inverse_low = split(inverse.T)
+    weights = jnp.concatenate([inverse_high, inverse_high, inverse_low], axis=0)
+    arrive(3)
+    core = lax.dot_general(triple(collect(3), 0), weights, (((0,), (0,)), ((), ())), preferred_element_type=jnp.float32)
     for c in range(local_three):
         for b in range(local_two):
             core_ref[b, c] = core[(c * local_two + b) * rank_four:(c * local_two + b + 1) * rank_four, :]
 
-    for stage in range(2):
-        wait_for(dealt.at[stage, pl.ds(0, (devices - 1) * tile)], send_sem.at[stage])
-        wait_for(dealt.at[stage, pl.ds(0, (devices - 1) * tile)], send_sem.at[2 + stage])
-    for h in range(2):
-        wait_for(paired.at[h], image_sem.at[0, h])
-        wait_for(shares.at[h, pl.ds(0, members - 1)], image_sem.at[2, h])
-        wait_for(shares.at[h, pl.ds(0, members - 1)], image_sem.at[4, h])
-        wait_for(paired.at[h], image_sem.at[6, h])
+    for stage in range(4):
+        wait_for(gots.at[stage, pl.ds(0, (devices - 1) * tile)], send_sem.at[stage])
+    wait_for(paired, image_sem.at[0])
+    wait_for(paired, image_sem.at[2])
+    for j in range(each):
+        wait_for(shares.at[j], share_sem.at[0, j])
+        wait_for(shares.at[j], share_sem.at[2, j])
     wait_for(twos.at[pl.ds(0, rows - 1)], factor_sem.at[0])
     wait_for(threes.at[pl.ds(0, cols - 1)], factor_sem.at[2])
 
@@ -494,10 +510,10 @@
     rank_one = factor_init.shape[1]
     local_three = width // fourth_len
     same = factor_two.shape[1] == local_two * rows and factor_three.shape[1] == local_three * cols
-    even = rows % 2 == 0 and cols % 2 == 0 and rank_one % 16 == 0 and rank_one % devices == 0
+    even = rows % 2 == 0 and cols % 2 == 0 and rank_one % devices == 0
     flat = local_two * rank_four == LANES and width == LANES and local_three * (rank_one // devices) == 8
-    tiles = (rank_one // 16) * (first_len // LANES)
-    return same and even and flat and first_len % (4 * LANES) == 0 and tiles % devices == 0 and (first_len // LANES) % (tiles // devices) == 0
+    tiles = (rank_one // 8) * (first_len // LANES)
+    return same and even and flat and first_len % (4 * LANES) == 0 and tiles % devices == 0
 
 
 def fused(tensor, factor_two, factor_three, factor_four, factor_init):
@@ -512,7 +528,7 @@
     features = local_three * lanes
     total_width = local_two * width
     tile = local_three * (rank_one // devices)
-    each = (rank_one // 16) * (first_len // LANES) // devices
+    each = (rank_one // 8) * (first_len // LANES) // devices
     wide = rows * lanes
 
     def f32(*shape):
@@ -537,15 +553,15 @@
             bf16(first_len, total_width), bf16(first_len, total_width), bf16(total_width, features), bf16(total_width, features),
             bf16(first_len, features), bf16(first_len, features), bf16(features, first_len), bf16(features, first_len),
             bf16(wide, wide), bf16(wide, wide), f32(rows, *factor_two.shape), f32(cols, *factor_three.shape),
-            f32(2, 2, members * tile, lanes), f32(2, devices * tile, lanes), f32(2, devices * tile, lanes), f32(2, 2, members * tile, lanes),
-            f32(2, 2, members, each, 8, LANES), f32(2, members, each, 8, LANES), f32(2, members, each, 8, LANES), f32(2, members, each, 8, LANES),
-            f32(2, each, 8, LANES), f32(2, 2, members, each, 8, LANES),
+            f32(4, devices * tile, lanes), f32(4, devices * tile, lanes),
+            f32(each, members, 8, LANES), f32(each, members, 8, LANES), f32(each, members, 8, LANES), f32(each, members, 8, LANES),
+            f32(each, 8, LANES), f32(2, each, members, 8, LANES),
             pltpu.SemaphoreType.DMA((local_two + 4,)),
             pltpu.SemaphoreType.DMA((4,)),
             pltpu.SemaphoreType.DMA((4,)),
-            pltpu.SemaphoreType.DMA((2,)),
-            pltpu.SemaphoreType.DMA((2, 2)),
-            pltpu.SemaphoreType.DMA((8, 2)),
+            pltpu.SemaphoreType.DMA((4,)),
+            pltpu.SemaphoreType.DMA((4,)),
+            pltpu.SemaphoreType.DMA((4, each)),
         ],
         compiler_params=pltpu.CompilerParams(collective_id=0, has_side_effects=True, vmem_limit_bytes=48 << 20),
     )(*operands)

time: 47.2 us -> 45.5 us (0.964)
  Pallas kernels: 46.3 us -> 44.2 us
    pallas_call x1, Pallas kernels: 45.5 us -> 43.4 us  [fused(): pl.pallas_call(hooi_kernel, out_shape=tuple((pltpu.VMEM(x.shape, x.dtype)...]
where the time goes in v3:
time: 45.5 us; the launch traced here: 44.9 us
  Pallas kernels  44.2 us (97%)
  between operations  0.64 us (1%)
    pallas_call x1, Pallas kernels, fused(): pl.pallas_call(hooi_kernel, out_shape=tuple((pltpu.VMEM(x.shape, x.dtype)...  43.4 us

profile of v3, /device:TPU:0, one launch (start us, length us, event | category | flops | bytes accessed | tf_op | source)
XLA Modules:
  0.0 44.9 jit_solution(7521576174832532852)
XLA Ops:
  0.6 43.4 %shard_map.68 = (f32[8,4,16,64]{3,2,1,0:T(8,128)S(1)}, f32[64,1024]{1,0:T(8,128)S(1)}) custom-call(f32[1024,8,128]{2,1,0:T(8,128)} %tensor_hbm.1, f32[8,32]{1,0:T(8,128)} %two_hbm.1, f32[4,32]{1,0:T(4,128)} %three_hbm.1, f32[16,32]{1,0:T(8,128)} %bitcast.5, f32[64,1024]{1,0:T(8,128)} %bitcast.4), custom_call_target="tpu_custom_call" | custom-call | tf_op jit(solution)/shard_map/pallas_call | solution.py:546
  44.1 0.8 %shard_map.69 = (f32[8,4,16,64]{3,2,1,0:T(8,128)}, f32[64,1024]{1,0:T(8,128)}) custom-call(f32[8,4,16,64]{3,2,1,0:T(8,128)S(1)} %get-tuple-element.6.core_ref, f32[64,1024]{1,0:T(8,128)S(1)} %get-tuple-element.7.basis_ref), custom_call_target="tpu_custom_call" | custom-call | tf_op jit(solution)/shard_map/pallas_call | solution.py:568

commit v4 on v3

--- a/solution.py
+++ b/solution.py
@@ -161,14 +161,6 @@
 
 def ones_where(mask):
     return jnp.where(mask, 1.0, 0.0).astype(jnp.float32)
-
-
-def expand_rows(square, copies):
-    tall = (square.shape[0] * copies, square.shape[0])
-    wide = (square.shape[1], square.shape[1] * copies)
-    result = dot(ones_where(iota(tall, 0) // copies == iota(tall, 1)), square, ((1,), (0,)))
-    result = dot(result, ones_where(iota(wide, 1) // copies == iota(wide, 0)), ((1,), (0,)))
-    return jnp.where(iota(result.shape, 0) % copies == iota(result.shape, 1) % copies, result, 0.0)
 
 
 def store_lanes(matrix, copies, high_ref, low_ref):
@@ -233,8 +225,6 @@
     lanes = local_two * rank_four
     features = local_three * lanes
     copies = rank_one // devices
-    tile = local_three * copies
-    each = sums.shape[0]
     spans = half_len // LANES
 
     slab_loads = [pltpu.make_async_copy(tensor_hbm.at[:, b, :], slabs.at[b], load_sem.at[b]) for b in range(local_two)]
@@ -262,7 +252,7 @@
         pl.semaphore_signal(barrier, inc=1, device_id=(there_row, there_col), device_id_type=pl.DeviceIdType.MESH)
 
     def hello(k, carry):
-        there_row, there_col = target(members - 1 - rows // 2 - k)
+        there_row, there_col = target(k)
         greet_at(there_row * 2, there_col)
         greet_at(there_row * 2 + 1, there_col)
         return carry
@@ -271,8 +261,8 @@
         greet_at(lax.rem(row + k, rows), col)
         return carry
 
-    lax.fori_loop(0, members - rows // 2, hello, 0)
-    lax.fori_loop(1, rows, hello_near, 0)
+    lax.fori_loop(0, members - rows // 2, hello, 0, unroll=True)
+    lax.fori_loop(1, rows, hello_near, 0, unroll=True)
 
     small_loads[0].wait()
     lane = iota((fourth_len, features), 1)
@@ -290,83 +280,74 @@
     small_loads[1].wait()
     init_high, init_low = split(init_ref[...])
     init_both = jnp.concatenate([init_high, init_low], axis=0)
-    group = 4 if local_two % 4 == 0 else 1
-    count = local_two // group
+    cuts = [0, local_two // 2, local_two]
+    count = len(cuts) - 1
+
+    def span_of(k):
+        return slice(cuts[k] * width, cuts[k + 1] * width)
 
     def pull_group(k):
-        part = slice(k * group * width, (k + 1) * group * width)
-        both = narrow(init_both, high_ref[:, part])
-        return both[:rank_one] + both[rank_one:] + narrow(init_high, low_ref[:, part])
-
-    def mix_group(k, pulled):
-        part = slice(k * group * width, (k + 1) * group * width)
-        return left_split(pulled, mix_high[part, :], mix_low[part, :])
+        both = narrow(init_both, high_ref[:, span_of(k)])
+        return both[:rank_one] + both[rank_one:] + narrow(init_high, low_ref[:, span_of(k)])
 
     pulled, vectors = [], []
     for k in range(count + 2):
         if k < count:
-            for b in range(k * group, (k + 1) * group):
+            for b in range(cuts[k], cuts[k + 1]):
                 slab_loads[b].wait()
                 high, low = split(slabs[b])
                 high_ref[:, b * width:(b + 1) * width] = high
                 low_ref[:, b * width:(b + 1) * width] = low
         if k >= 2:
-            vectors.append(mix_group(k - 2, pulled[k - 2]))
+            vectors.append(left_split(pulled[k - 2], mix_high[span_of(k - 2), :], mix_low[span_of(k - 2), :]))
         if 1 <= k <= count:
             pulled.append(pull_group(k - 1))
     vectors = sum(vectors[1:], vectors[0])
 
+    def flat(ref):
+        return ref.reshape(devices * local_three, lanes)
+
     def deal(vectors, put):
         for c in range(local_three):
-            for k in range(copies):
-                put[pl.ds(c * copies + k, devices, stride=tile), :] = vectors[k * devices:(k + 1) * devices, c * lanes:(c + 1) * lanes]
-
-    def send(stage):
-        put, got = puts.at[stage], gots.at[stage]
+            put[pl.ds(c, devices, stride=local_three), :] = vectors[:, c * lanes:(c + 1) * lanes]
+
+    def send(stage, k):
+        put, got = puts.at[stage, k], gots.at[stage, k]
 
         def one(there_row, there_col):
-            copy_to(put.at[at(there_row * cols + there_col, tile)], got.at[at(me, tile)], there_row, there_col, send_sem.at[stage], recv_sem.at[stage])
-
-        def some(k, carry):
-            there_row, there_col = target(lax.rem(k, members - 1))
-            one(there_row * 2 + k // (members - 1), there_col)
-            return carry
-
-        def both(k, carry):
-            there_row, there_col = target(k)
-            one(there_row * 2, there_col)
-            one(there_row * 2 + 1, there_col)
-            return carry
-
-        if stage in (0, 1, 2, 3):
-            lax.fori_loop(0, 2 * (members - 1), some, 0, unroll=5 if (members - 1) % 5 == 0 else 1)
-        else:
-            lax.fori_loop(0, members - 1, both, 0, unroll=3 if (members - 1) % 3 == 0 else 1)
+            copy_to(put.at[there_row * cols + there_col], got.at[me], there_row, there_col, send_sem.at[stage, k], recv_sem.at[stage, k])
+
+        for h in range(2):
+            def some(i, carry):
+                there_row, there_col = target(i)
+                one(there_row * 2 + h, there_col)
+                return carry
+
+            lax.fori_loop(0, members - 1, some, 0, unroll=True)
         one(partner, col)
-        here = at(me, tile)
-        got[here, :] = put[here, :]
-
-    def arrive(stage):
-        wait_for(gots.at[stage, pl.ds(0, (devices - 1) * tile)], recv_sem.at[stage])
-
-    def contract(stage, matrix):
-        block = jnp.concatenate([gots[stage, k * cols * tile:(k + 1) * cols * tile, :] for k in range(rows)], axis=1)
-        top, rest = split(block)
+        got[me] = put[me]
+
+    def arrive(stage, k):
+        wait_for(gots.at[stage, k, pl.ds(0, devices - 1)], recv_sem.at[stage, k])
+
+    def contract(stage, k, matrix):
+        got, put = flat(gots.at[stage, k]), flat(puts.at[stage + 1, k])
+        size = cols * local_three
+        top, rest = split(jnp.concatenate([got[i * size:(i + 1) * size, :] for i in range(rows)], axis=1))
         result = left_split(narrow(matrix, jnp.concatenate([top, top, rest], axis=0)), lane_high[...], lane_low[...])
-        for k in range(rows):
-            puts[stage + 1, k * cols * tile:(k + 1) * cols * tile, :] = result[:, k * lanes:(k + 1) * lanes]
+        for i in range(rows):
+            put[i * size:(i + 1) * size, :] = result[:, i * lanes:(i + 1) * lanes]
 
     def triple(matrix, axis):
         high, low = split(matrix)
         return jnp.concatenate([high, low, high], axis=axis)
 
-    def collect(stage):
-        got = gots.at[stage]
-        return jnp.concatenate([
-            jnp.concatenate([got[pl.ds(c * copies + k, devices, stride=tile), :] for k in range(copies)], axis=0)
-            for c in range(local_three)], axis=1)
-
-    deal(vectors, puts.at[0])
+    def collect(stage, k):
+        got = flat(gots.at[stage, k])
+        return jnp.concatenate([got[pl.ds(c, devices, stride=local_three), :] for c in range(local_three)], axis=1)
+
+    for k in range(copies):
+        deal(vectors[k * devices:(k + 1) * devices], flat(puts.at[0, k]))
     small_loads[2].wait()
     small_loads[3].wait()
     pl.semaphore_wait(barrier, devices - 1)
@@ -379,9 +360,10 @@
         copy_to(three_ref, threes.at[col], row, lax.rem(col + k, cols), factor_sem.at[2], factor_sem.at[3])
         return carry
 
-    lax.fori_loop(1, rows, send_two, 0)
-    lax.fori_loop(1, cols, send_three, 0)
-    send(0)
+    lax.fori_loop(1, rows, send_two, 0, unroll=True)
+    lax.fori_loop(1, cols, send_three, 0, unroll=True)
+    for k in range(copies):
+        send(0, k)
     twos[row] = two_ref[...]
     threes[col] = three_ref[...]
 
@@ -392,103 +374,110 @@
         turn_high[:, part], turn_low[:, part] = split(hat.T)
 
     hat_piece(0, 4)
-    hat_piece(1, 4)
     wait_for(twos.at[pl.ds(0, rows - 1)], factor_sem.at[1])
     wait_for(threes.at[pl.ds(0, cols - 1)], factor_sem.at[3])
     whole_two = jnp.concatenate([twos[k] for k in range(rows)], axis=0)
     whole_three = jnp.concatenate([threes[k] for k in range(cols)], axis=0)
     store_lanes(dot(whole_two, whole_two, ((1,), (1,))), rank_four, lane_high, lane_low)
-    left = triple(expand_rows(dot(whole_three, whole_three, ((1,), (1,))), copies), 1)
-
-    arrive(0)
-    contract(0, left)
-    send(1)
+    left = triple(dot(whole_three, whole_three, ((1,), (1,))), 1)
+
+    for k in range(copies):
+        arrive(0, k)
+        contract(0, k, left)
+        send(1, k)
+    hat_piece(1, 4)
     hat_piece(2, 4)
     hat_piece(3, 4)
 
-    arrive(1)
-    back = collect(1)
-
-    def image_part(which):
-        span = at(which, half_len)
-        return left_split(back, turn_high[:, span], turn_low[:, span])
-
     def tiles():
         for i in range(members):
-            for j in range(each):
-                r, w = (i * each + j) // spans, (i * each + j) % spans
-                yield i, j, slice(r * 8, (r + 1) * 8), slice(w * LANES, (w + 1) * LANES)
-
-    image = image_part(1 - half)
-    for i, j, r, w in tiles():
-        parts[j, i] = image[r, w]
-    copy_to(parts, paired, partner, col, image_sem.at[0], image_sem.at[1])
-    image = image_part(half)
-    wait_for(paired, image_sem.at[1])
-    for i, j, r, w in tiles():
-        sums[j, i] = image[r, w] + paired[j, i]
-
-    for j in range(each):
-        def scatter(k, carry):
-            there_row, there_col = target(k)
-            copy_to(sums.at[j, there_row * cols + there_col], shares.at[j, seat], there_row * 2 + 1 - half, there_col, share_sem.at[0, j], share_sem.at[1, j])
+            r, w = i // spans, i % spans
+            yield i, slice(r * 8, (r + 1) * 8), slice(w * LANES, (w + 1) * LANES)
+
+    owned = []
+    for k in range(copies):
+        arrive(1, k)
+        back = collect(1, k)
+        span = at(1 - half, half_len)
+        image = left_split(back, turn_high[:, span], turn_low[:, span])
+        for i, r, w in tiles():
+            parts[k, i] = image[r, w]
+        copy_to(parts.at[k], paired.at[k], partner, col, share_sem.at[4, k], share_sem.at[5, k])
+        span = at(half, half_len)
+        owned.append(left_split(back, turn_high[:, span], turn_low[:, span]))
+
+    for k in range(copies):
+        wait_for(paired.at[k], share_sem.at[5, k])
+        for i, r, w in tiles():
+            sums[k, i] = owned[k][r, w] + paired[k, i]
+
+        def scatter(i, carry):
+            there_row, there_col = target(i)
+            copy_to(sums.at[k, there_row * cols + there_col], shares.at[k, seat], there_row * 2 + 1 - half, there_col, share_sem.at[0, k], share_sem.at[1, k])
             return carry
 
-        lax.fori_loop(0, members, scatter, 0, unroll=4)
-    for j in range(each):
-        wait_for(shares.at[j], share_sem.at[1, j])
-        mine[j] = jnp.sum(shares[j], axis=0)
-
-        def gather(k, carry):
-            there_row, there_col = target(k)
-            copy_to(mine.at[j], spread.at[1 - half, j, seat], there_row * 2 + 1 - half, there_col, share_sem.at[2, j], share_sem.at[3, j])
+        lax.fori_loop(0, members, scatter, 0, unroll=True)
+    for k in range(copies):
+        wait_for(shares.at[k], share_sem.at[1, k])
+        mine[k] = jnp.sum(shares[k], axis=0)
+
+        def gather(i, carry):
+            there_row, there_col = target(i)
+            copy_to(mine.at[k], spread.at[1 - half, k, seat], there_row * 2 + 1 - half, there_col, share_sem.at[2, k], share_sem.at[3, k])
             return carry
 
-        lax.fori_loop(0, members, gather, 0, unroll=4)
-    for j in range(each):
-        wait_for(spread.at[half, j], share_sem.at[3, j])
-        copy_to(spread.at[half, j], spread.at[half, j], partner, col, image_sem.at[2], image_sem.at[3])
-
-    def image_half(which):
+        lax.fori_loop(0, members, gather, 0, unroll=True)
+    def image_half(which, k):
         return jnp.concatenate([
-            jnp.concatenate([spread[which, (r * spans + w) % each, (r * spans + w) // each] for w in range(spans)], axis=1)
-            for r in range(rank_one // 8)], axis=0)
-
-    def pull_half(which):
+            jnp.concatenate([spread[which, k, r * spans + w] for w in range(spans)], axis=1)
+            for r in range(members // spans)], axis=0)
+
+    def pull_half(which, k):
         span = at(which, half_len)
-        return left_split(image_half(which), hat_high[span, :], hat_low[span, :])
-
-    vectors = pull_half(half)
-    wait_for(spread.at[1 - half], image_sem.at[3])
-    deal(vectors + pull_half(1 - half), puts.at[2])
-    send(2)
-
-    image = jnp.concatenate([image_half(0), image_half(1)], axis=1)
+        return left_split(image_half(which, k), hat_high[span, :], hat_low[span, :])
+
+    def pass_on(k):
+        wait_for(spread.at[half, k], share_sem.at[3, k])
+        copy_to(spread.at[half, k], spread.at[half, k], partner, col, image_sem.at[0, k], image_sem.at[1, k])
+
+    pass_on(0)
+    for k in range(copies):
+        vectors = pull_half(half, k)
+        if k + 1 < copies:
+            pass_on(k + 1)
+        wait_for(spread.at[1 - half, k], image_sem.at[1, k])
+        deal(vectors + pull_half(1 - half, k), flat(puts.at[2, k]))
+        send(2, k)
+
+    image = jnp.concatenate([jnp.concatenate([image_half(0, k), image_half(1, k)], axis=1) for k in range(copies)], axis=0)
     lower = dot(image, image, ((1,), (1,)))
     shape = lower.shape
     lower, inverse = eliminate(lower, ones_where(iota(shape, 0) == iota(shape, 1)), 0, rank_one * 5 // 8)
     store_lanes(whole_two, rank_four, lane_high, lane_low)
-    left = triple(expand_rows(whole_three.T, copies), 1)
-    arrive(2)
-    contract(2, left)
-    send(3)
+    left = triple(whole_three.T, 1)
+    for k in range(copies):
+        arrive(2, k)
+        contract(2, k, left)
+        send(3, k)
     lower, inverse = eliminate(lower, inverse, rank_one * 5 // 8, rank_one)
     basis_ref[...] = dot(inverse, image, ((1,), (0,)))
     inverse_high, inverse_low = split(inverse.T)
     weights = jnp.concatenate([inverse_high, inverse_high, inverse_low], axis=0)
-    arrive(3)
-    core = lax.dot_general(triple(collect(3), 0), weights, (((0,), (0,)), ((), ())), preferred_element_type=jnp.float32)
+    for k in range(copies):
+        arrive(3, k)
+    vectors = jnp.concatenate([collect(3, k) for k in range(copies)], axis=0)
+    core = lax.dot_general(triple(vectors, 0), weights, (((0,), (0,)), ((), ())), preferred_element_type=jnp.float32)
     for c in range(local_three):
         for b in range(local_two):
             core_ref[b, c] = core[(c * local_two + b) * rank_four:(c * local_two + b + 1) * rank_four, :]
 
-    for stage in range(4):
-        wait_for(gots.at[stage, pl.ds(0, (devices - 1) * tile)], send_sem.at[stage])
-    wait_for(paired, image_sem.at[0])
-    wait_for(paired, image_sem.at[2])
-    for j in range(each):
-        wait_for(shares.at[j], share_sem.at[0, j])
-        wait_for(shares.at[j], share_sem.at[2, j])
+    for k in range(copies):
+        for stage in range(4):
+            wait_for(gots.at[stage, k, pl.ds(0, devices - 1)], send_sem.at[stage, k])
+        wait_for(paired.at[k], share_sem.at[4, k])
+        wait_for(shares.at[k], share_sem.at[0, k])
+        wait_for(shares.at[k], share_sem.at[2, k])
+        wait_for(paired.at[k], image_sem.at[0, k])
     wait_for(twos.at[pl.ds(0, rows - 1)], factor_sem.at[0])
     wait_for(threes.at[pl.ds(0, cols - 1)], factor_sem.at[2])
 
@@ -511,9 +500,9 @@
     local_three = width // fourth_len
     same = factor_two.shape[1] == local_two * rows and factor_three.shape[1] == local_three * cols
     even = rows % 2 == 0 and cols % 2 == 0 and rank_one % devices == 0
-    flat = local_two * rank_four == LANES and width == LANES and local_three * (rank_one // devices) == 8
-    tiles = (rank_one // 8) * (first_len // LANES)
-    return same and even and flat and first_len % (4 * LANES) == 0 and tiles % devices == 0
+    flat = local_two * rank_four == LANES and width == LANES and (local_three == 4 or local_three % 8 == 0)
+    tiles = (devices // 8) * (first_len // (2 * LANES))
+    return same and even and flat and first_len % (4 * LANES) == 0 and devices % 8 == 0 and tiles == devices // 2
 
 
 def fused(tensor, factor_two, factor_three, factor_four, factor_init):
@@ -527,8 +516,7 @@
     lanes = local_two * rank_four
     features = local_three * lanes
     total_width = local_two * width
-    tile = local_three * (rank_one // devices)
-    each = (rank_one // 8) * (first_len // LANES) // devices
+    copies = rank_one // devices
     wide = rows * lanes
 
     def f32(*shape):
@@ -553,15 +541,15 @@
             bf16(first_len, total_width), bf16(first_len, total_width), bf16(total_width, features), bf16(total_width, features),
             bf16(first_len, features), bf16(first_len, features), bf16(features, first_len), bf16(features, first_len),
             bf16(wide, wide), bf16(wide, wide), f32(rows, *factor_two.shape), f32(cols, *factor_three.shape),
-            f32(4, devices * tile, lanes), f32(4, devices * tile, lanes),
-            f32(each, members, 8, LANES), f32(each, members, 8, LANES), f32(each, members, 8, LANES), f32(each, members, 8, LANES),
-            f32(each, 8, LANES), f32(2, each, members, 8, LANES),
+            f32(4, copies, devices, local_three, lanes), f32(4, copies, devices, local_three, lanes),
+            f32(copies, members, 8, LANES), f32(copies, members, 8, LANES), f32(copies, members, 8, LANES), f32(copies, members, 8, LANES),
+            f32(copies, 8, LANES), f32(2, copies, members, 8, LANES),
             pltpu.SemaphoreType.DMA((local_two + 4,)),
             pltpu.SemaphoreType.DMA((4,)),
-            pltpu.SemaphoreType.DMA((4,)),
-            pltpu.SemaphoreType.DMA((4,)),
-            pltpu.SemaphoreType.DMA((4,)),
-            pltpu.SemaphoreType.DMA((4, each)),
+            pltpu.SemaphoreType.DMA((4, copies)),
+            pltpu.SemaphoreType.DMA((4, copies)),
+            pltpu.SemaphoreType.DMA((2, copies)),
+            pltpu.SemaphoreType.DMA((6, copies)),
         ],
         compiler_params=pltpu.CompilerParams(collective_id=0, has_side_effects=True, vmem_limit_bytes=48 << 20),
     )(*operands)

time: 45.5 us -> 44.6 us (0.980); the launches traced: 44.9 us -> 44.4 us
  no operation moved by 1% of the time
where the time goes in v4:
time: 44.6 us; the launch traced here: 44.4 us
  Pallas kernels  43.8 us (98%)
  between operations  0.64 us (1%)
    pallas_call x1, Pallas kernels, fused(): pl.pallas_call(hooi_kernel, out_shape=tuple((pltpu.VMEM(x.shape, x.dtype)...  43 us

profile of v4, /device:TPU:0, one launch (start us, length us, event | category | flops | bytes accessed | tf_op | source)
XLA Modules:
  0.0 44.4 jit_solution(18149620121207335608)
XLA Ops:
  0.6 43.0 %shard_map.68 = (f32[8,4,16,64]{3,2,1,0:T(8,128)S(1)}, f32[64,1024]{1,0:T(8,128)S(1)}) custom-call(f32[1024,8,128]{2,1,0:T(8,128)} %tensor_hbm.1, f32[8,32]{1,0:T(8,128)} %two_hbm.1, f32[4,32]{1,0:T(4,128)} %three_hbm.1, f32[16,32]{1,0:T(8,128)} %bitcast.5, f32[64,1024]{1,0:T(8,128)} %bitcast.4), custom_call_target="tpu_custom_call" | custom-call | tf_op jit(solution)/shard_map/pallas_call | solution.py:534
  43.6 0.8 %shard_map.69 = (f32[8,4,16,64]{3,2,1,0:T(8,128)}, f32[64,1024]{1,0:T(8,128)}) custom-call(f32[8,4,16,64]{3,2,1,0:T(8,128)S(1)} %get-tuple-element.6.core_ref, f32[64,1024]{1,0:T(8,128)S(1)} %get-tuple-element.7.basis_ref), custom_call_target="tpu_custom_call" | custom-call | tf_op jit(solution)/shard_map/pallas_call | solution.py:556

commit v5 on v4

--- a/solution.py
+++ b/solution.py
@@ -304,6 +304,13 @@
             pulled.append(pull_group(k - 1))
     vectors = sum(vectors[1:], vectors[0])
 
+    def fenced(body):
+        def trip(_, carry):
+            body()
+            return carry
+
+        lax.fori_loop(0, 1 + me // devices, trip, 0)
+
     def flat(ref):
         return ref.reshape(devices * local_three, lanes)
 
@@ -317,14 +324,14 @@
         def one(there_row, there_col):
             copy_to(put.at[there_row * cols + there_col], got.at[me], there_row, there_col, send_sem.at[stage, k], recv_sem.at[stage, k])
 
-        for h in range(2):
-            def some(i, carry):
-                there_row, there_col = target(i)
-                one(there_row * 2 + h, there_col)
-                return carry
-
-            lax.fori_loop(0, members - 1, some, 0, unroll=True)
-        one(partner, col)
+        @fenced
+        def _():
+            for h in range(2):
+                for i in range(members - 1):
+                    there_row, there_col = target(i)
+                    one(there_row * 2 + h, there_col)
+            one(partner, col)
+
         got[me] = put[me]
 
     def arrive(stage, k):
@@ -394,39 +401,51 @@
             r, w = i // spans, i % spans
             yield i, slice(r * 8, (r + 1) * 8), slice(w * LANES, (w + 1) * LANES)
 
-    owned = []
-    for k in range(copies):
-        arrive(1, k)
+    def image_part(back, which):
+        span = at(which, half_len)
+        return left_split(back, turn_high[:, span], turn_low[:, span])
+
+    def image_out(k):
         back = collect(1, k)
-        span = at(1 - half, half_len)
-        image = left_split(back, turn_high[:, span], turn_low[:, span])
+        image = image_part(back, 1 - half)
         for i, r, w in tiles():
             parts[k, i] = image[r, w]
-        copy_to(parts.at[k], paired.at[k], partner, col, share_sem.at[4, k], share_sem.at[5, k])
-        span = at(half, half_len)
-        owned.append(left_split(back, turn_high[:, span], turn_low[:, span]))
-
-    for k in range(copies):
+        fenced(lambda: copy_to(parts.at[k], paired.at[k], partner, col, share_sem.at[4, k], share_sem.at[5, k]))
+        return back
+
+    def scatter(k, image):
         wait_for(paired.at[k], share_sem.at[5, k])
         for i, r, w in tiles():
-            sums[k, i] = owned[k][r, w] + paired[k, i]
-
-        def scatter(i, carry):
-            there_row, there_col = target(i)
-            copy_to(sums.at[k, there_row * cols + there_col], shares.at[k, seat], there_row * 2 + 1 - half, there_col, share_sem.at[0, k], share_sem.at[1, k])
-            return carry
-
-        lax.fori_loop(0, members, scatter, 0, unroll=True)
+            sums[k, i] = image[r, w] + paired[k, i]
+
+        @fenced
+        def _():
+            for i in range(members):
+                there_row, there_col = target(i)
+                copy_to(sums.at[k, there_row * cols + there_col], shares.at[k, seat], there_row * 2 + 1 - half, there_col, share_sem.at[0, k], share_sem.at[1, k])
+
+    arrive(1, 0)
+    owned = image_part(image_out(0), half)
+    for k in range(copies):
+        if k + 1 < copies:
+            arrive(1, k + 1)
+            back = image_out(k + 1)
+        scatter(k, owned)
+        if k + 1 < copies:
+            owned = image_part(back, half)
+
+    store_lanes(whole_two, rank_four, lane_high, lane_low)
+    left = triple(whole_three.T, 1)
     for k in range(copies):
         wait_for(shares.at[k], share_sem.at[1, k])
         mine[k] = jnp.sum(shares[k], axis=0)
 
-        def gather(i, carry):
-            there_row, there_col = target(i)
-            copy_to(mine.at[k], spread.at[1 - half, k, seat], there_row * 2 + 1 - half, there_col, share_sem.at[2, k], share_sem.at[3, k])
-            return carry
-
-        lax.fori_loop(0, members, gather, 0, unroll=True)
+        @fenced
+        def _():
+            for i in range(members):
+                there_row, there_col = target(i)
+                copy_to(mine.at[k], spread.at[1 - half, k, seat], there_row * 2 + 1 - half, there_col, share_sem.at[2, k], share_sem.at[3, k])
+
     def image_half(which, k):
         return jnp.concatenate([
             jnp.concatenate([spread[which, k, r * spans + w] for w in range(spans)], axis=1)
@@ -438,7 +457,7 @@
 
     def pass_on(k):
         wait_for(spread.at[half, k], share_sem.at[3, k])
-        copy_to(spread.at[half, k], spread.at[half, k], partner, col, image_sem.at[0, k], image_sem.at[1, k])
+        fenced(lambda: copy_to(spread.at[half, k], spread.at[half, k], partner, col, image_sem.at[0, k], image_sem.at[1, k]))
 
     pass_on(0)
     for k in range(copies):
@@ -452,14 +471,12 @@
     image = jnp.concatenate([jnp.concatenate([image_half(0, k), image_half(1, k)], axis=1) for k in range(copies)], axis=0)
     lower = dot(image, image, ((1,), (1,)))
     shape = lower.shape
-    lower, inverse = eliminate(lower, ones_where(iota(shape, 0) == iota(shape, 1)), 0, rank_one * 5 // 8)
-    store_lanes(whole_two, rank_four, lane_high, lane_low)
-    left = triple(whole_three.T, 1)
+    lower, inverse = eliminate(lower, ones_where(iota(shape, 0) == iota(shape, 1)), 0, rank_one * 3 // 8)
     for k in range(copies):
         arrive(2, k)
         contract(2, k, left)
         send(3, k)
-    lower, inverse = eliminate(lower, inverse, rank_one * 5 // 8, rank_one)
+    lower, inverse = eliminate(lower, inverse, rank_one * 3 // 8, rank_one)
     basis_ref[...] = dot(inverse, image, ((1,), (0,)))
     inverse_high, inverse_low = split(inverse.T)
     weights = jnp.concatenate([inverse_high, inverse_high, inverse_low], axis=0)

time: 44.6 us -> 43.1 us (0.966)
  Pallas kernels: 43.8 us -> 42.2 us
    pallas_call x1, Pallas kernels: 43 us -> 41.4 us  [fused(): pl.pallas_call(hooi_kernel, out_shape=tuple((pltpu.VMEM(x.shape, x.dtype)...]
where the time goes in v5:
time: 43.1 us; the launch traced here: 42.9 us
  Pallas kernels  42.2 us (98%)
  between operations  0.64 us (1%)
    pallas_call x1, Pallas kernels, fused(): pl.pallas_call(hooi_kernel, out_shape=tuple((pltpu.VMEM(x.shape, x.dtype)...  41.4 us

profile of v5, /device:TPU:0, one launch (start us, length us, event | category | flops | bytes accessed | tf_op | source)
XLA Modules:
  0.0 42.9 jit_solution(2578392767255202720)
XLA Ops:
  0.6 41.4 %shard_map.68 = (f32[8,4,16,64]{3,2,1,0:T(8,128)S(1)}, f32[64,1024]{1,0:T(8,128)S(1)}) custom-call(f32[1024,8,128]{2,1,0:T(8,128)} %tensor_hbm.1, f32[8,32]{1,0:T(8,128)} %two_hbm.1, f32[4,32]{1,0:T(4,128)} %three_hbm.1, f32[16,32]{1,0:T(8,128)} %bitcast.5, f32[64,1024]{1,0:T(8,128)} %bitcast.4), custom_call_target="tpu_custom_call" | custom-call | tf_op jit(solution)/shard_map/pallas_call | solution.py:551
  42.1 0.8 %shard_map.69 = (f32[8,4,16,64]{3,2,1,0:T(8,128)}, f32[64,1024]{1,0:T(8,128)}) custom-call(f32[8,4,16,64]{3,2,1,0:T(8,128)S(1)} %get-tuple-element.6.core_ref, f32[64,1024]{1,0:T(8,128)S(1)} %get-tuple-element.7.basis_ref), custom_call_target="tpu_custom_call" | custom-call | tf_op jit(solution)/shard_map/pallas_call | solution.py:573

commit v6 on v5

--- a/solution.py
+++ b/solution.py
@@ -237,11 +237,13 @@
     small_loads[2].start()
     small_loads[3].start()
 
-    def target(k):
-        turn = k // (rows // 2)
-        shift = (turn + 1) // 2
-        there = lax.rem(col + cols // 2 + cols + (1 - 2 * lax.rem(turn, 2)) * shift, cols)
-        return lax.rem(row // 2 + rows - 1 - lax.rem(k, rows // 2), rows // 2), there
+    pairs = cols // 2
+    turns = sorted(range(pairs), key=lambda z: (z == 0, -abs(2 * z - pairs)))
+    away = [d for d in [(near, far, flip) for flip in (1, 0) for near in reversed(range(rows // 2)) for far in turns] if any(d)]
+
+    def there(distance):
+        near, far, flip = distance
+        return lax.rem(row // 2 + near, rows // 2), lax.rem(col // 2 + far, pairs) * 2 + lax.rem(col + flip, 2)
 
     def at(index, count):
         return pl.ds(pl.multiple_of(index * count, count), count)
@@ -251,18 +253,11 @@
     def greet_at(there_row, there_col):
         pl.semaphore_signal(barrier, inc=1, device_id=(there_row, there_col), device_id_type=pl.DeviceIdType.MESH)
 
-    def hello(k, carry):
-        there_row, there_col = target(k)
+    for distance in away:
+        there_row, there_col = there(distance)
         greet_at(there_row * 2, there_col)
         greet_at(there_row * 2 + 1, there_col)
-        return carry
-
-    def hello_near(k, carry):
-        greet_at(lax.rem(row + k, rows), col)
-        return carry
-
-    lax.fori_loop(0, members - rows // 2, hello, 0, unroll=True)
-    lax.fori_loop(1, rows, hello_near, 0, unroll=True)
+    greet_at(partner, col)
 
     small_loads[0].wait()
     lane = iota((fourth_len, features), 1)
@@ -327,8 +322,8 @@
         @fenced
         def _():
             for h in range(2):
-                for i in range(members - 1):
-                    there_row, there_col = target(i)
+                for distance in away:
+                    there_row, there_col = there(distance)
                     one(there_row * 2 + h, there_col)
             one(partner, col)
 
@@ -420,8 +415,8 @@
 
         @fenced
         def _():
-            for i in range(members):
-                there_row, there_col = target(i)
+            for distance in away + [(0, 0, 0)]:
+                there_row, there_col = there(distance)
                 copy_to(sums.at[k, there_row * cols + there_col], shares.at[k, seat], there_row * 2 + 1 - half, there_col, share_sem.at[0, k], share_sem.at[1, k])
 
     arrive(1, 0)
@@ -442,8 +437,8 @@
 
         @fenced
         def _():
-            for i in range(members):
-                there_row, there_col = target(i)
+            for distance in away + [(0, 0, 0)]:
+                there_row, there_col = there(distance)
                 copy_to(mine.at[k], spread.at[1 - half, k, seat], there_row * 2 + 1 - half, there_col, share_sem.at[2, k], share_sem.at[3, k])
 
     def image_half(which, k):
@@ -479,11 +474,13 @@
     lower, inverse = eliminate(lower, inverse, rank_one * 3 // 8, rank_one)
     basis_ref[...] = dot(inverse, image, ((1,), (0,)))
     inverse_high, inverse_low = split(inverse.T)
-    weights = jnp.concatenate([inverse_high, inverse_high, inverse_low], axis=0)
+    core = None
     for k in range(copies):
         arrive(3, k)
-    vectors = jnp.concatenate([collect(3, k) for k in range(copies)], axis=0)
-    core = lax.dot_general(triple(vectors, 0), weights, (((0,), (0,)), ((), ())), preferred_element_type=jnp.float32)
+        part = slice(k * devices, (k + 1) * devices)
+        weights = jnp.concatenate([inverse_high[part], inverse_high[part], inverse_low[part]], axis=0)
+        more = lax.dot_general(triple(collect(3, k), 0), weights, (((0,), (0,)), ((), ())), preferred_element_type=jnp.float32)
+        core = more if core is None else core + more
     for c in range(local_three):
         for b in range(local_two):
             core_ref[b, c] = core[(c * local_two + b) * rank_four:(c * local_two + b + 1) * rank_four, :]

time: 43.1 us -> 40.4 us (0.937)
  Pallas kernels: 42.2 us -> 39.5 us
    pallas_call x1, Pallas kernels: 41.4 us -> 38.7 us  [fused(): pl.pallas_call(hooi_kernel, out_shape=tuple((pltpu.VMEM(x.shape, x.dtype)...]
where the time goes in v6:
time: 40.4 us; the launch traced here: 40.2 us
  Pallas kernels  39.5 us (98%)
  between operations  0.64 us (2%)
    pallas_call x1, Pallas kernels, fused(): pl.pallas_call(hooi_kernel, out_shape=tuple((pltpu.VMEM(x.shape, x.dtype)...  38.7 us
    pallas_call x1, Pallas kernels, fused(): pl.pallas_call(write_kernel, out_shape=shapes, in_specs=[vmem, vmem], out...  0.81 us

profile of v6, /device:TPU:0, one launch (start us, length us, event | category | flops | bytes accessed | tf_op | source)
XLA Modules:
  0.0 40.2 jit_solution(13539081712197618139)
XLA Ops:
  0.6 38.7 %shard_map.68 = (f32[8,4,16,64]{3,2,1,0:T(8,128)S(1)}, f32[64,1024]{1,0:T(8,128)S(1)}) custom-call(f32[1024,8,128]{2,1,0:T(8,128)} %tensor_hbm.1, f32[8,32]{1,0:T(8,128)} %two_hbm.1, f32[4,32]{1,0:T(4,128)} %three_hbm.1, f32[16,32]{1,0:T(8,128)} %bitcast.5, f32[64,1024]{1,0:T(8,128)} %bitcast.4), custom_call_target="tpu_custom_call" | custom-call | tf_op jit(solution)/shard_map/pallas_call | solution.py:548
  39.4 0.8 %shard_map.69 = (f32[8,4,16,64]{3,2,1,0:T(8,128)}, f32[64,1024]{1,0:T(8,128)}) custom-call(f32[8,4,16,64]{3,2,1,0:T(8,128)S(1)} %get-tuple-element.6.core_ref, f32[64,1024]{1,0:T(8,128)S(1)} %get-tuple-element.7.basis_ref), custom_call_target="tpu_custom_call" | custom-call | tf_op jit(solution)/shard_map/pallas_call | solution.py:570

commit v7 on v6

--- a/solution.py
+++ b/solution.py
@@ -321,10 +321,12 @@
 
         @fenced
         def _():
-            for h in range(2):
-                for distance in away:
-                    there_row, there_col = there(distance)
-                    one(there_row * 2 + h, there_col)
+            for flip in (1, 0):
+                for h in range(2):
+                    for distance in away:
+                        if distance[2] == flip:
+                            there_row, there_col = there(distance)
+                            one(there_row * 2 + h, there_col)
             one(partner, col)
 
         got[me] = put[me]

time: 40.4 us -> 40.3 us (level)
  no operation moved by 1% of the time
where the time goes in v7:
time: 40.3 us; the launch traced here: 40.1 us
  Pallas kernels  39.4 us (98%)
  between operations  0.64 us (2%)
    pallas_call x1, Pallas kernels, fused(): pl.pallas_call(hooi_kernel, out_shape=tuple((pltpu.VMEM(x.shape, x.dtype)...  38.6 us
    pallas_call x1, Pallas kernels, fused(): pl.pallas_call(write_kernel, out_shape=shapes, in_specs=[vmem, vmem], out...  0.81 us

profile of v7, /device:TPU:0, one launch (start us, length us, event | category | flops | bytes accessed | tf_op | source)
XLA Modules:
  0.0 40.1 jit_solution(12213961635339487225)
XLA Ops:
  0.6 38.6 %shard_map.68 = (f32[8,4,16,64]{3,2,1,0:T(8,128)S(1)}, f32[64,1024]{1,0:T(8,128)S(1)}) custom-call(f32[1024,8,128]{2,1,0:T(8,128)} %tensor_hbm.1, f32[8,32]{1,0:T(8,128)} %two_hbm.1, f32[4,32]{1,0:T(4,128)} %three_hbm.1, f32[16,32]{1,0:T(8,128)} %bitcast.5, f32[64,1024]{1,0:T(8,128)} %bitcast.4), custom_call_target="tpu_custom_call" | custom-call | tf_op jit(solution)/shard_map/pallas_call | solution.py:550
  39.3 0.8 %shard_map.69 = (f32[8,4,16,64]{3,2,1,0:T(8,128)}, f32[64,1024]{1,0:T(8,128)}) custom-call(f32[8,4,16,64]{3,2,1,0:T(8,128)S(1)} %get-tuple-element.6.core_ref, f32[64,1024]{1,0:T(8,128)S(1)} %get-tuple-element.7.basis_ref), custom_call_target="tpu_custom_call" | custom-call | tf_op jit(solution)/shard_map/pallas_call | solution.py:572
